TPU v7x, 32 devices: a whole 2x2x4 slice. The times are simulated.
32 devices in a mesh: gx: 8 (over y, x, core), gy: 4 (over z).
Axes of the slice: x: 2, y: 2, z: 4, core: 2. Of those that a mesh axis runs over, the one named last changes fastest.
Arguments:
- features: bfloat16 [32, 16, 128, 128], P(None, 'gx', 'gy'), may hold values from -80 to 80
- kernel_one: bfloat16 [32, 32, 3, 3, 3], replicated, may hold values from -0.21875 to 0.21875
- gain_one: float32 [32], replicated, may hold values from 0.5 to 1.5
- bias_one: float32 [32], replicated, may hold values from -0.5 to 0.5
- kernel_two: bfloat16 [32, 32, 3, 3, 3], replicated, may hold values from -0.21875 to 0.21875
- gain_two: float32 [32], replicated, may hold values from 0.5 to 1.5
- bias_two: float32 [32], replicated, may hold values from -0.5 to 0.5
- cotangent: bfloat16 [32, 16, 128, 128], P(None, 'gx', 'gy'), may hold values from -80 to 80
Outputs:
- output: bfloat16 [32, 16, 128, 128], P(None, 'gx', 'gy')
- features_grad: bfloat16 [32, 16, 128, 128], P(None, 'gx', 'gy')
- kernel_one_grad: float32 [32, 32, 3, 3, 3], replicated
- kernel_two_grad: float32 [32, 32, 3, 3, 3], replicated
- norm_grads: float32 [4, 32], replicated
All inputs are finite; a program needn't handle non-finite values.
Results may differ from a plain program's by a relative error of at most 0.0078.
Values may be sent and summed in bfloat16 or wider, within the bound.
A program may use at most 192 MiB of HBM per device.

v0:
```python
import jax
import jax.numpy as jnp
from jax import lax
from jax.sharding import PartitionSpec as P

EPSILON = 1e-05
SLOPE = 0.01
SHARPNESS = 8.0


def extended(block, sides, width):
    for axis, dim in sides:
        count = lax.axis_size(axis)
        forward = [(i, i + 1) for i in range(count - 1)]
        backward = [(target, source) for source, target in forward]
        low = lax.ppermute(
            lax.slice_in_dim(block, block.shape[dim] - width, None, axis=dim), axis, forward
        )
        high = lax.ppermute(lax.slice_in_dim(block, 0, width, axis=dim), axis, backward)
        block = jnp.concatenate([low, block, high], axis=dim)
    return block


def activate(shifted):
    return SLOPE * shifted + (1.0 - SLOPE) * jax.nn.softplus(SHARPNESS * shifted) / SHARPNESS


def activate_slope(shifted):
    return SLOPE + (1.0 - SLOPE) * jax.nn.sigmoid(SHARPNESS * shifted)


def column(values):
    return values[:, None, None, None]


def pad_depth(values, margin):
    return jnp.pad(values, ((0, 0), (0, 0), (0, 0), (margin, margin)))


def conv_valid(padded, kernel):
    size_x = padded.shape[1] - 2
    size_y = padded.shape[2] - 2
    size_z = padded.shape[3] - 2
    total = jnp.zeros((kernel.shape[0], size_x, size_y, size_z), jnp.float32)
    for off_x in range(3):
        for off_y in range(3):
            for off_z in range(3):
                window = padded[
                    :, off_x : off_x + size_x, off_y : off_y + size_y, off_z : off_z + size_z
                ]
                total = total + jnp.einsum(
                    "oi,ixyz->oxyz",
                    kernel[:, :, off_x, off_y, off_z],
                    window,
                    preferred_element_type=jnp.float32,
                )
    return total


def flip_kernel(kernel):
    return jnp.transpose(kernel[:, :, ::-1, ::-1, ::-1], (1, 0, 2, 3, 4))


def weight_grad(padded, gradient):
    size_x = gradient.shape[1]
    size_y = gradient.shape[2]
    size_z = gradient.shape[3]
    pieces = []
    for off_x in range(3):
        for off_y in range(3):
            for off_z in range(3):
                window = padded[
                    :, off_x : off_x + size_x, off_y : off_y + size_y, off_z : off_z + size_z
                ]
                pieces.append(
                    jnp.einsum(
                        "oxyz,ixyz->oi", gradient, window, preferred_element_type=jnp.float32
                    )
                )
    stacked = jnp.stack(pieces, axis=-1)
    return stacked.reshape(gradient.shape[0], padded.shape[0], 3, 3, 3)


def face_cells(values):
    return pad_depth(extended(values, (("gx", 1), ("gy", 2)), 1), 1)


def gradient_cells(values):
    return pad_depth(extended(values, (("gx", 1), ("gy", 2)), 1), 1)


def sum_weights(local_terms):
    return lax.psum(local_terms, ("gx", "gy"))


def channel_stats(hidden, total_cells):
    sums, squares = lax.psum(
        (jnp.sum(hidden, axis=(1, 2, 3)), jnp.sum(jnp.square(hidden), axis=(1, 2, 3))), ("gx", "gy")
    )
    center = sums / total_cells
    spread = squares / total_cells - jnp.square(center)
    return (center, lax.rsqrt(spread + EPSILON))


def norm_backward(slope, normed, gain, inverse_std, total_cells):
    sum_plain, sum_normed = lax.psum(
        (jnp.sum(slope, axis=(1, 2, 3)), jnp.sum(slope * normed, axis=(1, 2, 3))), ("gx", "gy")
    )
    gradient = column(gain * inverse_std) * (
        slope - column(sum_plain / total_cells) - normed * column(sum_normed / total_cells)
    )
    return (gradient.astype(jnp.bfloat16), sum_plain, sum_normed)


def local(features, kernel_one, gain_one, bias_one, kernel_two, gain_two, bias_two, cotangent):
    rows_x = features.shape[1]
    rows_y = features.shape[2]
    total_cells = float(
        rows_x * rows_y * features.shape[3] * lax.axis_size("gx") * lax.axis_size("gy")
    )
    x_pad = face_cells(features)
    hidden_one = conv_valid(x_pad, kernel_one)
    center_one, inv_one = channel_stats(hidden_one, total_cells)
    normed_one = (hidden_one - column(center_one)) * column(inv_one)
    shifted_one = normed_one * column(gain_one) + column(bias_one)
    a_pad = face_cells(activate(shifted_one).astype(jnp.bfloat16))
    hidden_two = conv_valid(a_pad, kernel_two)
    center_two, inv_two = channel_stats(hidden_two, total_cells)
    normed_two = (hidden_two - column(center_two)) * column(inv_two)
    shifted_two = normed_two * column(gain_two) + column(bias_two)
    output = activate(shifted_two).astype(jnp.bfloat16)
    slope_two = cotangent.astype(jnp.float32) * activate_slope(shifted_two)
    grad_two, plain_two, nsum_two = norm_backward(
        slope_two, normed_two, gain_two, inv_two, total_cells
    )
    scale = 1.0 / jnp.sqrt(jnp.float32(total_cells))
    local_two = weight_grad(a_pad, grad_two)
    summed_two = sum_weights(local_two)
    back_one = conv_valid(gradient_cells(grad_two), flip_kernel(kernel_two))
    slope_one = back_one * activate_slope(shifted_one)
    grad_one, plain_one, nsum_one = norm_backward(
        slope_one, normed_one, gain_one, inv_one, total_cells
    )
    local_one = weight_grad(x_pad, grad_one)
    summed_one = sum_weights(local_one)
    features_grad = conv_valid(gradient_cells(grad_one), flip_kernel(kernel_one)).astype(
        jnp.bfloat16
    )
    norm_grads = jnp.stack([nsum_one, plain_one, nsum_two, plain_two]) * scale
    return (output, features_grad, summed_one * scale, summed_two * scale, norm_grads)


def solution(mesh):
    in_specs = (P(None, "gx", "gy", None), P(), P(), P(), P(), P(), P(), P(None, "gx", "gy", None))
    out_specs = (P(None, "gx", "gy", None), P(None, "gx", "gy", None), P(), P(), P())
    return jax.shard_map(local, mesh=mesh, in_specs=in_specs, out_specs=out_specs, check_vma=False)
```

profile of v0, /device:TPU:0, one launch (start us, length us, event | category | flops | bytes accessed | tf_op | source)
XLA Modules:
  0.0 467.0 jit_solution(14253346436259396878)
XLA Ops:
  7.2 1.5 copy.13
  8.7 0.8 fusion.516
  9.5 2.4 collective-permute-start
  11.9 1.3 collective-permute-start.1
  13.4 0.7 reverse_bitcast_fusion.1
  14.3 0.7 reverse_bitcast_fusion
  15.0 0.4 fusion.408
  15.9 1.8 collective-permute-done.1
  17.7 3.5 collective-permute-start.2
  21.2 1.3 collective-permute-start.3
  23.1 3.9 collective-permute-done.3
  27.0 1.2 fusion.8
  34.1 1.1 fusion.108
  36.1 2.0 fusion.511
  38.1 43.7 %all-reduce.7 = (f32[32]{0:T(128)S(1)}, f32[32]{0:T(128)S(1)}) all-reduce(f32[32]{0:T(128)S(1)} %get-tuple-element.17, f32[32]{0:T(128)S(1)} %get-tuple-element.16), channel_id=1, replica_groups=mesh['gx'=8,'gy'=4] {'gx','gy'}, use_global_device_ids=true, to_apply=%region_3.4 | all-reduce | flops 64 | bytes 512 | tf_op jit(solution)/shard_map/psum | solution.py:97
  81.9 0.5 fusion.481
  82.4 2.2 fusion.170
  84.6 1.4 collective-permute-start.4
  86.1 1.3 collective-permute-start.5
  87.4 1.0 fusion.380
  88.4 3.6 collective-permute-done.5
  92.0 2.2 collective-permute-start.6
  94.2 1.3 collective-permute-start.7
  96.0 3.9 collective-permute-done.7
  100.8 2.1 select_maximum_fusion.8
  108.7 1.0 fusion.109
  110.1 2.4 fusion.510
  112.5 44.0 %all-reduce.6 = (f32[32]{0:T(128)}, f32[32]{0:T(128)}) all-reduce(f32[32]{0:T(128)} %get-tuple-element.15, f32[32]{0:T(128)S(1)} %get-tuple-element.14), channel_id=1, replica_groups=mesh['gx'=8,'gy'=4] {'gx','gy'}, use_global_device_ids=true, to_apply=%region_7.8 | all-reduce | flops 64 | bytes 512 | tf_op jit(solution)/shard_map/psum | solution.py:97
  156.5 1.3 fusion.480
  157.7 0.5 copy-done.35
  158.3 4.6 fusion.509
  162.9 40.0 %all-reduce.5 = (f32[32]{0:T(128)}, f32[32]{0:T(128)}) all-reduce(f32[32]{0:T(128)} %get-tuple-element.13, f32[32]{0:T(128)} %get-tuple-element.12), channel_id=1, replica_groups=mesh['gx'=8,'gy'=4] {'gx','gy'}, use_global_device_ids=true, to_apply=%region_11.12 | all-reduce | flops 64 | bytes 512 | tf_op jit(solution)/shard_map/psum | solution.py:106
  202.9 0.8 broadcast_multiply_fusion.4
  203.7 2.0 multiply_convert_fusion.1
  206.0 1.3 collective-permute-start.8
  207.3 1.3 collective-permute-start.9
  216.4 0.4 fusion.114
  216.8 1.0 copy.23
  218.1 3.8 collective-permute-start.10
  221.9 1.5 collective-permute-start.11
  223.9 3.8 collective-permute-done.11
  228.4 2.1 select_maximum_fusion.4
  236.4 1.0 fusion.110
  237.7 0.8 copy-done.6
  238.6 2.3 fusion.508
  240.9 43.7 %all-reduce.4 = (f32[32]{0:T(128)S(1)}, f32[32]{0:T(128)S(1)}) all-reduce(f32[32]{0:T(128)S(1)} %get-tuple-element.11, f32[32]{0:T(128)S(1)} %get-tuple-element.10), channel_id=1, replica_groups=mesh['gx'=8,'gy'=4] {'gx','gy'}, use_global_device_ids=true, to_apply=%region_15.16 | all-reduce | flops 64 | bytes 512 | tf_op jit(solution)/shard_map/psum | solution.py:106
  284.5 1.9 multiply_convert_fusion
  286.7 0.9 fusion.513
  291.6 0.5 fusion.154
  294.9 0.4 fusion.144
  296.2 1.3 collective-permute-start.12
  297.5 1.3 collective-permute-start.13
  298.8 1.3 fusion.365
  300.2 0.6 maximum_multiply_fusion
  300.7 132.9 %all-reduce.11.cloned.1.call-done = (f32[32,32,3,3,3]{1,0,4,3,2:T(8,128)}, f32[32,32,3,3,3]{1,0,4,3,2:T(8,128)}) async-done(((f32[32,32,3,3,3]{1,0,4,3,2:T(8,128)}, f32[32,32,3,3,3]{1,0,4,3,2:T(8,128)}), (f32[32,32,3,3,3]{1,0,4,3,2:T(8,128)}, f32[32,32,3,3,3]{1,0,4,3,2:T(8,128)})) %all-reduce.11.cloned.1.call-update) | async-done | bytes 221200 | tf_op jit(solution)/shard_map/psum | solution.py:93
  433.7 1.8 broadcast_multiply_fusion
  435.5 1.8 broadcast_multiply_fusion.1
  437.3 4.2 collective-permute-start.14
  441.5 1.5 collective-permute-start.15
  443.6 3.7 collective-permute-done.15
  448.0 2.1 select_maximum_fusion
  456.3 1.0 fusion.111
  457.7 1.0 fusion.113
  458.7 1.0 copy.24
  (256 shorter events, 47.1 us)
Async XLA Ops:
  7.2 7.9 %copy-start.13 = (bf16[32,2,32,128]{3,2,1,0:T(8,128)(2,1)S(1)}, bf16[32,2,32,128]{3,2,1,0:T(8,128)(2,1)}, u32[]{:S(2)}) copy-start(bf16[32,2,32,128]{3,2,1,0:T(8,128)(2,1)} %param.8) | copy-start | bytes 1572868
  7.2 6.1 %copy-start.26 = (bf16[32,32,3,3,3]{1,0,4,3,2:T(8,128)(2,1)S(1)}, bf16[32,32,3,3,3]{1,0,4,3,2:T(8,128)(2,1)}, u32[]{:S(2)}) copy-start(bf16[32,32,3,3,3]{1,0,4,3,2:T(8,128)(2,1)} %param.12) | copy-start | bytes 165892
  7.2 6.9 %copy-start.23 = (bf16[32,32,3,3,3]{1,0,4,3,2:T(8,128)(2,1)S(1)}, bf16[32,32,3,3,3]{1,0,4,3,2:T(8,128)(2,1)}, u32[]{:S(2)}) copy-start(bf16[32,32,3,3,3]{1,0,4,3,2:T(8,128)(2,1)} %param.9) | copy-start | bytes 165892
  7.2 426.5 %all-reduce.11.cloned.1.call-start = ((), (), s32[]{:S(2)}) async-start(), calls=%async_computation | async-start | bytes 1769472 | tf_op jit(solution)/shard_map/psum | solution.py:93
  8.7 14.1 %copy-start.7 = (bf16[32,2,32,128]{3,0,2,1:T(8,128)(2,1)}, bf16[32,2,32,128]{3,0,2,1:T(8,128)(2,1)S(1)}, u32[]{:S(2)}) copy-start(bf16[32,2,32,128]{3,0,2,1:T(8,128)(2,1)S(1)} %copy.13) | copy-start | bytes 1572868
  9.5 5.9 %collective-permute-start = (bf16[32,1,32,128]{3,0,2,1:T(8,128)(2,1)S(1)}, bf16[32,1,32,128]{3,0,2,1:T(8,128)(2,1)S(1)}, u32[]{:S(2)}, u32[]{:S(2)}) collective-permute-start(bf16[32,1,32,128]{3,0,2,1:T(8,128)(2,1)S(1)} %get-tuple-element.51), channel_id=1, source_target_pairs={{0,4},{4,8},{8,12},{12,16},{16,20},{20,24},{24,28},{1,5},{5,9},{9,... | collective-permute-start | bytes 786440 | tf_op jit(solution)/shard_map/ppermute | solution.py:16
  11.9 5.7 %collective-permute-start.1 = (bf16[32,1,32,128]{3,0,2,1:T(8,128)(2,1)}, bf16[32,1,32,128]{3,0,2,1:T(8,128)(2,1)S(1)}, u32[]{:S(2)}, u32[]{:S(2)}) collective-permute-start(bf16[32,1,32,128]{3,0,2,1:T(8,128)(2,1)} %get-tuple-element.50), channel_id=1, source_target_pairs={{4,0},{8,4},{12,8},{16,12},{20,16},{24,20},{28,24},{5,1},{9,5},{13... | collective-permute-start | bytes 786440 | tf_op jit(solution)/shard_map/ppermute | solution.py:19
  15.4 7.6 %copy-start.21 = (bf16[32,1,32,128]{3,0,2,1:T(8,128)(2,1)}, bf16[32,1,32,128]{3,0,2,1:T(8,128)(2,1)S(1)}, u32[]{:S(2)}) copy-start(bf16[32,1,32,128]{3,0,2,1:T(8,128)(2,1)S(1)} %collective-permute-done) | copy-start | bytes 786436
  17.7 5.4 %copy-start.19 = (bf16[32,1,32,128]{3,0,2,1:T(8,128)(2,1)}, bf16[32,1,32,128]{3,0,2,1:T(8,128)(2,1)S(1)}, u32[]{:S(2)}) copy-start(bf16[32,1,32,128]{3,0,2,1:T(8,128)(2,1)S(1)} %collective-permute-done.1) | copy-start | bytes 786436
  17.7 5.4 %collective-permute-start.2 = (bf16[32,4,1,128]{3,0,2,1:T(8,128)(2,1)S(1)}, bf16[32,4,1,128]{3,0,2,1:T(8,128)(2,1)S(1)}, u32[]{:S(2)}, u32[]{:S(2)}) collective-permute-start(bf16[32,4,1,128]{3,0,2,1:T(8,128)(2,1)S(1)} %get-tuple-element.42), channel_id=1, source_target_pairs={{0,1},{1,2},{2,3},{4,5},{5,6},{6,7},{8,9},{9,10},{10,11},{12,13},{... | collective-permute-start | bytes 98312 | tf_op jit(solution)/shard_map/ppermute | solution.py:16
  21.2 5.8 %collective-permute-start.3 = (bf16[32,4,1,128]{3,0,2,1:T(8,128)(2,1)S(1)}, bf16[32,4,1,128]{3,0,2,1:T(8,128)(2,1)S(1)}, u32[]{:S(2)}, u32[]{:S(2)}) collective-permute-start(bf16[32,4,1,128]{3,0,2,1:T(8,128)(2,1)S(1)} %get-tuple-element.43), channel_id=1, source_target_pairs={{1,0},{2,1},{3,2},{5,4},{6,5},{7,6},{9,8},{10,9},{11,10},{13,12},{... | collective-permute-start | bytes 98312 | tf_op jit(solution)/shard_map/ppermute | solution.py:19
  23.1 12.1 %copy-start.30 = (bf16[32,4,1,128]{3,0,2,1:T(8,128)(2,1)}, bf16[32,4,1,128]{3,0,2,1:T(8,128)(2,1)S(1)}, u32[]{:S(2)}) copy-start(bf16[32,4,1,128]{3,0,2,1:T(8,128)(2,1)S(1)} %collective-permute-done.2) | copy-start | bytes 98308
  27.0 8.8 %copy-start.28 = (bf16[32,4,1,128]{3,0,2,1:T(8,128)(2,1)}, bf16[32,4,1,128]{3,0,2,1:T(8,128)(2,1)S(1)}, u32[]{:S(2)}) copy-start(bf16[32,4,1,128]{3,0,2,1:T(8,128)(2,1)S(1)} %collective-permute-done.3) | copy-start | bytes 98308
  36.1 45.8 %copy-start.34 = (f32[32]{0:T(128)S(1)}, f32[32]{0:T(128)}, u32[]{:S(2)}) copy-start(f32[32]{0:T(128)} %param.10) | copy-start | bytes 388
  36.1 46.3 %copy-start.36 = (f32[32]{0:T(128)S(1)}, f32[32]{0:T(128)}, u32[]{:S(2)}) copy-start(f32[32]{0:T(128)} %param.11) | copy-start | bytes 388
  84.5 16.2 %copy-start.4 = (bf16[32,2,32,128]{3,0,2,1:T(8,128)(2,1)}, bf16[32,2,32,128]{3,0,2,1:T(8,128)(2,1)S(1)}, u32[]{:S(2)}) copy-start(bf16[32,2,32,128]{3,0,2,1:T(8,128)(2,1)S(1)} %fusion.170) | copy-start | bytes 1572868
  84.6 10.9 %copy-start.27 = (bf16[32,32,3,3,3]{1,0,4,3,2:T(8,128)(2,1)S(1)}, bf16[32,32,3,3,3]{1,0,4,3,2:T(8,128)(2,1)}, u32[]{:S(2)}) copy-start(bf16[32,32,3,3,3]{1,0,4,3,2:T(8,128)(2,1)} %param.12) | copy-start | bytes 165892
  84.6 3.7 collective-permute-start.4
  86.1 5.9 %collective-permute-start.5 = (bf16[32,1,32,128]{3,0,2,1:T(8,128)(2,1)S(1)}, bf16[32,1,32,128]{3,0,2,1:T(8,128)(2,1)S(1)}, u32[]{:S(2)}, u32[]{:S(2)}) collective-permute-start(bf16[32,1,32,128]{3,0,2,1:T(8,128)(2,1)S(1)} %get-tuple-element.49), channel_id=1, source_target_pairs={{4,0},{8,4},{12,8},{16,12},{20,16},{24,20},{28,24},{5,1},{9,5},{13... | collective-permute-start | bytes 786440 | tf_op jit(solution)/shard_map/ppermute | solution.py:19
  88.3 12.4 %copy-start.15 = (bf16[32,1,32,128]{3,0,2,1:T(8,128)(2,1)}, bf16[32,1,32,128]{3,0,2,1:T(8,128)(2,1)S(1)}, u32[]{:S(2)}) copy-start(bf16[32,1,32,128]{3,0,2,1:T(8,128)(2,1)S(1)} %collective-permute-done.4) | copy-start | bytes 786436
  92.0 4.0 collective-permute-start.6
  94.2 5.8 %collective-permute-start.7 = (bf16[32,4,1,128]{3,0,2,1:T(8,128)(2,1)S(1)}, bf16[32,4,1,128]{3,0,2,1:T(8,128)(2,1)S(1)}, u32[]{:S(2)}, u32[]{:S(2)}) collective-permute-start(bf16[32,4,1,128]{3,0,2,1:T(8,128)(2,1)S(1)} %get-tuple-element.41), channel_id=1, source_target_pairs={{1,0},{2,1},{3,2},{5,4},{6,5},{7,6},{9,8},{10,9},{11,10},{13,12},{... | collective-permute-start | bytes 98312 | tf_op jit(solution)/shard_map/ppermute | solution.py:19
  100.2 6.1 %copy-start.9 = (bf16[32,4,33,128]{3,0,2,1:T(8,128)(2,1)}, bf16[32,4,33,128]{3,0,2,1:T(8,128)(2,1)S(1)}, u32[]{:S(2)}) copy-start(bf16[32,4,33,128]{3,0,2,1:T(8,128)(2,1)S(1)} %get-tuple-element.39) | copy-start | bytes 3244036
  100.2 6.4 %copy-start.11 = (bf16[32,4,33,128]{3,0,2,1:T(8,128)(2,1)}, bf16[32,4,33,128]{3,0,2,1:T(8,128)(2,1)S(1)}, u32[]{:S(2)}) copy-start(bf16[32,4,33,128]{3,0,2,1:T(8,128)(2,1)S(1)} %get-tuple-element.38) | copy-start | bytes 3244036
  102.9 7.2 %copy-start = (bf16[32,4,34,130]{3,0,2,1:T(8,128)(2,1)}, bf16[32,4,34,130]{3,0,2,1:T(8,128)(2,1)S(1)}, u32[]{:S(2)}) copy-start(bf16[32,4,34,130]{3,0,2,1:T(8,128)(2,1)S(1)} %select_maximum_fusion.8) | copy-start | bytes 3394564
  157.7 0.5 copy-start.35
  202.9 2.8 copy-start.1
  203.7 4.9 %copy-start.12 = (bf16[32,4,33,128]{3,0,2,1:T(8,128)(2,1)S(1)}, bf16[32,4,33,128]{3,0,2,1:T(8,128)(2,1)}, u32[]{:S(2)}) copy-start(bf16[32,4,33,128]{3,0,2,1:T(8,128)(2,1)} %copy-done.11) | copy-start | bytes 3244036
  205.7 3.8 copy-start.5
  205.7 3.8 copy-start.16
  206.0 12.1 %collective-permute-start.8 = (bf16[32,1,32,128]{3,0,2,1:T(8,128)(2,1)S(1)}, bf16[32,1,32,128]{3,0,2,1:T(8,128)(2,1)S(1)}, u32[]{:S(2)}, u32[]{:S(2)}) collective-permute-start(bf16[32,1,32,128]{3,0,2,1:T(8,128)(2,1)S(1)} %get-tuple-element.46), channel_id=1, source_target_pairs={{0,4},{4,8},{8,12},{12,16},{16,20},{20,24},{24,28},{1,5},{5,9},{9,... | collective-permute-start | bytes 786440 | tf_op jit(solution)/shard_map/ppermute | solution.py:16
  207.3 10.8 %collective-permute-start.9 = (bf16[32,1,32,128]{3,0,2,1:T(8,128)(2,1)S(1)}, bf16[32,1,32,128]{3,0,2,1:T(8,128)(2,1)S(1)}, u32[]{:S(2)}, u32[]{:S(2)}) collective-permute-start(bf16[32,1,32,128]{3,0,2,1:T(8,128)(2,1)S(1)} %get-tuple-element.47), channel_id=1, source_target_pairs={{4,0},{8,4},{12,8},{16,12},{20,16},{24,20},{28,24},{5,1},{9,5},{13... | collective-permute-start | bytes 786440 | tf_op jit(solution)/shard_map/ppermute | solution.py:19
  209.3 1.2 copy-start.10
  215.5 1.3 copy-start.18
  215.8 2.0 copy-start.25
  216.8 6.8 %copy-start.32 = (f32[32,32,27]{1,0,2:T(8,128)}, f32[32,32,27]{1,0,2:T(8,128)S(1)}, u32[]{:S(2)}) copy-start(f32[32,32,27]{1,0,2:T(8,128)S(1)} %fusion.114) | copy-start | bytes 331780
  218.1 5.8 %collective-permute-start.10 = (bf16[32,4,1,128]{3,0,2,1:T(8,128)(2,1)S(1)}, bf16[32,4,1,128]{3,0,2,1:T(8,128)(2,1)S(1)}, u32[]{:S(2)}, u32[]{:S(2)}) collective-permute-start(bf16[32,4,1,128]{3,0,2,1:T(8,128)(2,1)S(1)} %get-tuple-element.36), channel_id=1, source_target_pairs={{0,1},{1,2},{2,3},{4,5},{5,6},{6,7},{8,9},{9,10},{10,11},{12,13},{... | collective-permute-start | bytes 98312 | tf_op jit(solution)/shard_map/ppermute | solution.py:16
  221.9 5.8 %collective-permute-start.11 = (bf16[32,4,1,128]{3,0,2,1:T(8,128)(2,1)S(1)}, bf16[32,4,1,128]{3,0,2,1:T(8,128)(2,1)S(1)}, u32[]{:S(2)}, u32[]{:S(2)}) collective-permute-start(bf16[32,4,1,128]{3,0,2,1:T(8,128)(2,1)S(1)} %get-tuple-element.37), channel_id=1, source_target_pairs={{1,0},{2,1},{3,2},{5,4},{6,5},{7,6},{9,8},{10,9},{11,10},{13,12},{... | collective-permute-start | bytes 98312 | tf_op jit(solution)/shard_map/ppermute | solution.py:19
  237.4 1.2 copy-start.6
  237.4 1.2 copy-start.37
  238.6 45.9 %copy-start.38 = (f32[32]{0:T(128)S(1)}, f32[32]{0:T(128)}, u32[]{:S(2)}) copy-start(f32[32]{0:T(128)} %get-tuple-element.52) | copy-start | bytes 388
  284.5 3.0 copy-start.31
  286.4 12.4 %copy-start.2 = (bf16[32,2,32,128]{3,0,2,1:T(8,128)(2,1)}, bf16[32,2,32,128]{3,0,2,1:T(8,128)(2,1)S(1)}, u32[]{:S(2)}) copy-start(bf16[32,2,32,128]{3,0,2,1:T(8,128)(2,1)S(1)} %multiply_convert_fusion) | copy-start | bytes 1572868
  287.5 1.0 copy-start.8
  287.6 1.1 copy-start.22
  288.2 1.4 copy-start.29
  290.5 1.1 copy-start.14
  293.4 1.2 copy-start.20
  294.9 4.0 copy-start.24
  295.5 4.6 copy-start.39
  295.5 4.6 copy-start.40
  296.2 3.9 copy-start.33
  296.2 141.1 %collective-permute-start.12 = (bf16[32,1,32,128]{3,0,2,1:T(8,128)(2,1)}, bf16[32,1,32,128]{3,0,2,1:T(8,128)(2,1)S(1)}, u32[]{:S(2)}, u32[]{:S(2)}) collective-permute-start(bf16[32,1,32,128]{3,0,2,1:T(8,128)(2,1)} %get-tuple-element.44), channel_id=1, source_target_pairs={{0,4},{4,8},{8,12},{12,16},{16,20},{20,24},{24,28},{1,5},{5,9},{9,... | collective-permute-start | bytes 786440 | tf_op jit(solution)/shard_map/ppermute | solution.py:16
  297.5 139.8 %collective-permute-start.13 = (bf16[32,1,32,128]{3,0,2,1:T(8,128)(2,1)}, bf16[32,1,32,128]{3,0,2,1:T(8,128)(2,1)S(1)}, u32[]{:S(2)}, u32[]{:S(2)}) collective-permute-start(bf16[32,1,32,128]{3,0,2,1:T(8,128)(2,1)} %get-tuple-element.45), channel_id=1, source_target_pairs={{4,0},{8,4},{12,8},{16,12},{20,16},{24,20},{28,24},{5,1},{9,5},{13... | collective-permute-start | bytes 786440 | tf_op jit(solution)/shard_map/ppermute | solution.py:19
  300.1 137.2 %copy-start.3 = (bf16[32,2,32,128]{3,0,2,1:T(8,128)(2,1)S(1)}, bf16[32,2,32,128]{3,0,2,1:T(8,128)(2,1)}, u32[]{:S(2)}) copy-start(bf16[32,2,32,128]{3,0,2,1:T(8,128)(2,1)} %copy-done.2) | copy-start | bytes 1572868
  437.3 6.3 %collective-permute-start.14 = (bf16[32,4,1,128]{3,0,2,1:T(8,128)(2,1)S(1)}, bf16[32,4,1,128]{3,0,2,1:T(8,128)(2,1)S(1)}, u32[]{:S(2)}, u32[]{:S(2)}) collective-permute-start(bf16[32,4,1,128]{3,0,2,1:T(8,128)(2,1)S(1)} %get-tuple-element.32), channel_id=1, source_target_pairs={{0,1},{1,2},{2,3},{4,5},{5,6},{6,7},{8,9},{9,10},{10,11},{12,13},{... | collective-permute-start | bytes 98312 | tf_op jit(solution)/shard_map/ppermute | solution.py:16
  441.5 5.8 %collective-permute-start.15 = (bf16[32,4,1,128]{3,0,2,1:T(8,128)(2,1)S(1)}, bf16[32,4,1,128]{3,0,2,1:T(8,128)(2,1)S(1)}, u32[]{:S(2)}, u32[]{:S(2)}) collective-permute-start(bf16[32,4,1,128]{3,0,2,1:T(8,128)(2,1)S(1)} %get-tuple-element.33), channel_id=1, source_target_pairs={{1,0},{2,1},{3,2},{5,4},{6,5},{7,6},{9,8},{10,9},{11,10},{13,12},{... | collective-permute-start | bytes 98312 | tf_op jit(solution)/shard_map/ppermute | solution.py:19
  455.1 1.2 copy-start.17
Sparse Core Ops, SparseCore 0:
  300.3 133.3 all-reduce.10
where the time goes:
time: 476 us; the launch traced here: 467 us
  blocking collectives  171 us (36%)
  waiting for transfers between devices  154 us (32%)
  matrix products  60.4 us (13%)
  starting transfers between devices  30.8 us (6%)
  other arithmetic  25.5 us (5%)
  between operations  15.7 us (3%)
  local copies, waits for them, and re-layouts  9.54 us (2%)
    psum x1, waiting for transfers between devices, sum_weights(): return lax.psum(local_terms, ('gx', 'gy'))  133 us
    psum x2, blocking collectives, channel_stats(): lax.psum((jnp.sum(hidden, axis=(1, 2, 3)), jnp.sum(jnp.square(hidden), ax...  87.7 us
    psum x2, blocking collectives, norm_backward(): lax.psum((jnp.sum(slope, axis=(1, 2, 3)), jnp.sum(slope * normed, axis=(1...  83.7 us
    dot_general x108, matrix products, conv_valid(): jnp.einsum('oi,ixyz->oxyz', kernel[:, :, off_x, off_y, off_z], window, pr...  43.5 us
    ppermute x8, waiting for transfers between devices, extended(): lax.ppermute(lax.slice_in_dim(block, 0, width, axis=dim), axis, backward)  20.7 us
    ppermute x8, starting transfers between devices, extended(): lax.ppermute(lax.slice_in_dim(block, block.shape[dim] - width, None, axis...  20 us
    dot_general x54, matrix products, weight_grad(): jnp.einsum('oxyz,ixyz->oi', gradient, window, preferred_element_type=jnp....  16.9 us
    ppermute x8, starting transfers between devices, extended(): lax.ppermute(lax.slice_in_dim(block, 0, width, axis=dim), axis, backward)  10.8 us
  transfers between devices with their start and end apart: 17, of which 7 were waited for; matrix products, arithmetic and copies ran while one was open for 4% of the time, Pallas kernels for 0%

commit v1 on v0

v1 whole, which is shorter than its diff:
```python
import functools

import jax
import jax.numpy as jnp
from jax import lax
from jax.experimental import pallas as pl
from jax.experimental.pallas import tpu as pltpu
from jax.sharding import PartitionSpec as P

EPSILON = 1e-05
SLOPE = 0.01
SHARPNESS = 8.0
MESH = pl.DeviceIdType.MESH
F32 = jnp.float32
BF16 = jnp.bfloat16
VSPEC = pl.BlockSpec(memory_space=pltpu.VMEM)
DIRECTIONS = [(i, j) for i in (-1, 0, 1) for j in (-1, 0, 1) if (i, j) != (0, 0)]


def activate(shifted):
    scaled = SHARPNESS * shifted
    soft = jnp.maximum(scaled, 0.0) + jnp.log1p(jnp.exp(-jnp.abs(scaled)))
    return SLOPE * shifted + (1.0 - SLOPE) * soft / SHARPNESS


def activate_slope(shifted):
    return SLOPE + (1.0 - SLOPE) / (1.0 + jnp.exp(-SHARPNESS * shifted))


def halo_kernel(nx, ny, t_ref, o_ref, p_ref, send, recv):
    gx, gy = lax.axis_index("gx"), lax.axis_index("gy")
    X, Y = t_ref.shape[0], t_ref.shape[1]
    peers = [(lax.rem(gx + dx + nx, nx), lax.rem(gy + dy + ny, ny)) for dx, dy in DIRECTIONS]
    barrier = pltpu.get_barrier_semaphore()
    for peer in peers:
        pl.semaphore_signal(barrier, inc=1, device_id=peer, device_id_type=MESH)
    pl.semaphore_wait(barrier, len(peers))

    def source(d, size):
        return pl.ds(size - 1, 1) if d == 1 else (pl.ds(0, 1) if d == -1 else pl.ds(0, size))

    def target(d, size):
        return pl.ds(0, 1) if d == 1 else (pl.ds(size + 1, 1) if d == -1 else pl.ds(1, size))

    copies = []
    for k, (dx, dy) in enumerate(DIRECTIONS):
        copy = pltpu.make_async_remote_copy(
            src_ref=t_ref.at[source(dx, X), source(dy, Y)],
            dst_ref=p_ref.at[target(dx, X), target(dy, Y)],
            send_sem=send.at[k],
            recv_sem=recv.at[k],
            device_id=peers[k],
            device_id_type=MESH,
        )
        copy.start()
        copies.append(copy)
    o_ref[1 : X + 1, 1 : Y + 1] = t_ref[...]
    for copy in copies:
        copy.wait()
    low_x = jnp.where(gx > 0, 1.0, 0.0)
    high_x = jnp.where(gx < nx - 1, 1.0, 0.0)
    low_y = jnp.where(gy > 0, 1.0, 0.0)
    high_y = jnp.where(gy < ny - 1, 1.0, 0.0)

    def kept(values, flag):
        return (values.astype(F32) * flag).astype(BF16)

    o_ref[0, 1 : Y + 1] = kept(p_ref[0, 1 : Y + 1], low_x)
    o_ref[X + 1, 1 : Y + 1] = kept(p_ref[X + 1, 1 : Y + 1], high_x)
    for x in range(X + 2):
        side = low_x if x == 0 else (high_x if x == X + 1 else None)
        low = low_y if side is None else low_y * side
        high = high_y if side is None else high_y * side
        o_ref[x, 0] = kept(p_ref[x, 0], low)
        o_ref[x, Y + 1] = kept(p_ref[x, Y + 1], high)


def halo(block, nx, ny):
    X, Y, C, Z = block.shape
    return pl.pallas_call(
        functools.partial(halo_kernel, nx, ny),
        name="halo",
        out_shape=jax.ShapeDtypeStruct((X + 2, Y + 2, C, Z), block.dtype),
        in_specs=[VSPEC],
        out_specs=VSPEC,
        scratch_shapes=[
            pltpu.VMEM((X + 2, Y + 2, C, Z), block.dtype),
            pltpu.SemaphoreType.DMA((8,)),
            pltpu.SemaphoreType.DMA((8,)),
        ],
        compiler_params=pltpu.CompilerParams(collective_id=0, has_side_effects=True),
    )(block)


def greet(nx, ny, gx, gy):
    barrier = pltpu.get_barrier_semaphore()
    for k in range(1, nx):
        peer = (lax.rem(gx + k, nx), gy)
        pl.semaphore_signal(barrier, inc=1, device_id=peer, device_id_type=MESH)
    for k in range(1, ny):
        peer = (gx, lax.rem(gy + k, ny))
        pl.semaphore_signal(barrier, inc=1, device_id=peer, device_id_type=MESH)
    pl.semaphore_wait(barrier, nx + ny - 2)


def spread(count, me, peer_of, source_of, slots, send, recv):
    copies = []
    for k in range(1, count):
        other = lax.rem(me + k, count)
        copy = pltpu.make_async_remote_copy(
            src_ref=source_of(other),
            dst_ref=slots(me),
            send_sem=send.at[k],
            recv_sem=recv.at[me],
            device_id=peer_of(other),
            device_id_type=MESH,
        )
        copy.start()
        copies.append(copy)
    for k in range(1, count):
        other = lax.rem(me + k, count)
        pltpu.make_async_remote_copy(
            src_ref=source_of(other),
            dst_ref=slots(other),
            send_sem=send.at[k],
            recv_sem=recv.at[other],
            device_id=peer_of(other),
            device_id_type=MESH,
        ).wait_recv()
    for copy in copies:
        copy.wait_send()


def ordered_sum(ref, count):
    total = ref[0]
    for k in range(1, count):
        total = total + ref[k]
    return total


def stats_kernel(nx, ny, s_ref, o_ref, bx, by, mid, sx, rx, sy, ry):
    gx, gy = lax.axis_index("gx"), lax.axis_index("gy")
    greet(nx, ny, gx, gy)
    bx[gx] = s_ref[...]
    spread(nx, gx, lambda o: (o, gy), lambda o: s_ref, lambda i: bx.at[i], sx, rx)
    mid[...] = ordered_sum(bx, nx)
    by[gy] = mid[...]
    spread(ny, gy, lambda o: (gx, o), lambda o: mid, lambda i: by.at[i], sy, ry)
    o_ref[...] = ordered_sum(by, ny)


def sum_stats(local, nx, ny):
    R, L = local.shape
    return pl.pallas_call(
        functools.partial(stats_kernel, nx, ny),
        name="stats_sum",
        out_shape=jax.ShapeDtypeStruct((R, L), F32),
        in_specs=[VSPEC],
        out_specs=VSPEC,
        scratch_shapes=[
            pltpu.VMEM((nx, R, L), F32),
            pltpu.VMEM((ny, R, L), F32),
            pltpu.VMEM((R, L), F32),
            pltpu.SemaphoreType.DMA((nx,)),
            pltpu.SemaphoreType.DMA((nx,)),
            pltpu.SemaphoreType.DMA((ny,)),
            pltpu.SemaphoreType.DMA((ny,)),
        ],
        compiler_params=pltpu.CompilerParams(collective_id=1, has_side_effects=True),
    )(local)


def weights_kernel(nx, ny, s_ref, o_ref, bx, by, mid, fin, gat, sx, rx, sy, ry, sg, rg):
    gx, gy = lax.axis_index("gx"), lax.axis_index("gy")
    greet(nx, ny, gx, gy)
    bx[gx] = s_ref[gx]
    spread(nx, gx, lambda o: (o, gy), lambda o: s_ref.at[o], lambda i: bx.at[i], sx, rx)
    mid[...] = ordered_sum(bx, nx)
    by[gy] = mid[...]
    spread(ny, gy, lambda o: (gx, o), lambda o: mid, lambda i: by.at[i], sy, ry)
    fin[...] = ordered_sum(by, ny)
    gat[gx] = fin[...]
    spread(nx, gx, lambda o: (o, gy), lambda o: fin, lambda i: gat.at[i], sg, rg)
    o_ref[...] = gat[...]


def sum_weights(local, nx, ny):
    R, L = local.shape
    piece = -(-R // (8 * nx)) * 8
    split = jnp.pad(local, ((0, piece * nx - R), (0, 0))).reshape(nx, piece, L)
    summed = pl.pallas_call(
        functools.partial(weights_kernel, nx, ny),
        name="weights_sum",
        out_shape=jax.ShapeDtypeStruct((nx, piece, L), F32),
        in_specs=[VSPEC],
        out_specs=VSPEC,
        scratch_shapes=[
            pltpu.VMEM((nx, piece, L), F32),
            pltpu.VMEM((ny, piece, L), F32),
            pltpu.VMEM((piece, L), F32),
            pltpu.VMEM((piece, L), F32),
            pltpu.VMEM((nx, piece, L), F32),
            pltpu.SemaphoreType.DMA((nx,)),
            pltpu.SemaphoreType.DMA((nx,)),
            pltpu.SemaphoreType.DMA((ny,)),
            pltpu.SemaphoreType.DMA((ny,)),
            pltpu.SemaphoreType.DMA((nx,)),
            pltpu.SemaphoreType.DMA((nx,)),
        ],
        compiler_params=pltpu.CompilerParams(collective_id=2, has_side_effects=True),
    )(split)
    return summed.reshape(nx * piece, L)[:R]


def taps(row):
    wide = row.astype(F32)
    size = row.shape[1]
    lane = lax.broadcasted_iota(jnp.int32, wide.shape, 1)
    before = jnp.where(lane == 0, 0.0, pltpu.roll(wide, 1, 1)).astype(BF16)
    after = jnp.where(lane == size - 1, 0.0, pltpu.roll(wide, size - 1, 1)).astype(BF16)
    return jnp.concatenate([before, row, after], axis=0)


def conv_rows(p_ref, w_ref, acc_ref, v_ref=None, dw_ref=None):
    X = acc_ref.shape[0]
    C = acc_ref.shape[2]
    Z = acc_ref.shape[3]
    acc_ref[...] = jnp.zeros_like(acc_ref)
    if dw_ref is not None:
        dw_ref[...] = jnp.zeros_like(dw_ref)

    def body(j, carry):
        y = 2 * j
        for xp in range(X + 2):
            first, last = max(0, xp - (X - 1)), min(2, xp)
            pair = jnp.concatenate([taps(p_ref[xp, y]), taps(p_ref[xp, y + 1])], axis=1)
            part = jnp.dot(
                w_ref[first * 3 * C : (last + 1) * 3 * C, :], pair, preferred_element_type=F32
            )
            for dx in range(first, last + 1):
                base = (dx - first) * 3 * C
                one = [part[base + d * C : base + (d + 1) * C, :Z] for d in range(3)]
                two = [part[base + d * C : base + (d + 1) * C, Z:] for d in range(3)]
                x = xp - dx
                acc_ref[x, y] += one[2]
                acc_ref[x, y + 1] += one[1] + two[2]
                acc_ref[x, y + 2] += one[0] + two[1]
                acc_ref[x, y + 3] += two[0]
            if dw_ref is not None:
                left = []
                for dx in range(first, last + 1):
                    x = xp - dx
                    now = v_ref[x, pl.ds(y, 3)].reshape(3 * C, Z)
                    later = v_ref[x, pl.ds(y + 1, 3)].reshape(3 * C, Z)
                    left.append(jnp.concatenate([now, later], axis=1))
                left = left[0] if len(left) == 1 else jnp.concatenate(left, axis=0)
                dw_ref[first * 3 * C : (last + 1) * 3 * C, : 3 * C] += lax.dot_general(
                    left, pair, (((1,), (1,)), ((), ())), preferred_element_type=F32
                )
        return carry

    lax.fori_loop(0, p_ref.shape[1] // 2, body, 0)


def pack_pair(one, two):
    lane = lax.broadcasted_iota(jnp.int32, one.shape, 1)
    one = jnp.sum(one, axis=1, keepdims=True)
    two = jnp.sum(two, axis=1, keepdims=True)
    return jnp.where(lane == 0, one, jnp.where(lane == 1, two, 0.0))


def normal_terms(s_ref, total_cells):
    center = s_ref[:, 0:1] / total_cells
    spread_ = s_ref[:, 1:2] / total_cells - jnp.square(center)
    return center, lax.rsqrt(spread_ + EPSILON)


def rows(X, Y, step, carry):
    group = 4 if Y % 4 == 0 else 1

    def body(block, carry):
        for k in range(group):
            for x in range(X):
                carry = step(x, block * group + k, carry)
        return carry

    return lax.fori_loop(0, Y // group, body, carry)


def forward_kernel(p_ref, w_ref, h_ref, s_ref, acc_ref):
    X, Y, C, Z = h_ref.shape
    conv_rows(p_ref, w_ref, acc_ref)

    def step(x, y, carry):
        h = acc_ref[x, y + 2]
        h_ref[x, y] = h
        return carry[0] + h, carry[1] + h * h

    zero = jnp.zeros((C, Z), F32)
    s_ref[...] = pack_pair(*rows(X, Y, step, (zero, zero)))


def active_kernel(total_cells, h_ref, s_ref, gb_ref, a_ref):
    X, Y, C, Z = h_ref.shape
    center, inverse = normal_terms(s_ref, total_cells)
    gain, bias = gb_ref[0], gb_ref[1]

    def step(x, y, carry):
        shifted = (h_ref[x, y] - center) * inverse * gain + bias
        a_ref[x, y] = activate(shifted).astype(BF16)
        return carry

    rows(X, Y, step, 0)


def output_kernel(total_cells, h_ref, s_ref, gb_ref, c_ref, o_ref, t_ref):
    X, Y, C, Z = h_ref.shape
    center, inverse = normal_terms(s_ref, total_cells)
    gain, bias = gb_ref[0], gb_ref[1]

    def step(x, y, carry):
        normed = (h_ref[x, y] - center) * inverse
        shifted = normed * gain + bias
        o_ref[x, y] = activate(shifted).astype(BF16)
        slope = c_ref[x, y].astype(F32) * activate_slope(shifted)
        return carry[0] + slope, carry[1] + slope * normed

    zero = jnp.zeros((C, Z), F32)
    t_ref[...] = pack_pair(*rows(X, Y, step, (zero, zero)))


def gradient_kernel(total_cells, has_slope, h_ref, s_ref, gb_ref, c_ref, t_ref, g_ref):
    X, Y, C, Z = h_ref.shape
    center, inverse = normal_terms(s_ref, total_cells)
    gain, bias = gb_ref[0], gb_ref[1]
    plain = t_ref[:, 0:1] / total_cells
    along = t_ref[:, 1:2] / total_cells
    factor = gain * inverse

    def step(x, y, carry):
        normed = (h_ref[x, y] - center) * inverse
        slope = c_ref[x, y].astype(F32)
        if not has_slope:
            slope = slope * activate_slope(normed * gain + bias)
        g_ref[x, y] = (factor * (slope - plain - normed * along)).astype(BF16)
        return carry

    rows(X, Y, step, 0)


def fill_own(v_ref, own_ref):
    X, Y, C, Z = v_ref.shape
    edge = jnp.zeros((X, 2, C, Z), BF16)
    own_ref[:, 0:2] = edge
    own_ref[:, Y + 2 : Y + 4] = edge
    own_ref[:, 2 : Y + 2] = v_ref[...]


def back_kernel(
    total_cells, p_ref, v_ref, w_ref, h_ref, s_ref, gb_ref, o_ref, t_ref, dw_ref, acc_ref, own_ref
):
    X, Y, C, Z = o_ref.shape
    fill_own(v_ref, own_ref)
    conv_rows(p_ref, w_ref, acc_ref, own_ref, dw_ref)
    center, inverse = normal_terms(s_ref, total_cells)
    gain, bias = gb_ref[0], gb_ref[1]

    def step(x, y, carry):
        normed = (h_ref[x, y] - center) * inverse
        slope = acc_ref[x, y + 2] * activate_slope(normed * gain + bias)
        o_ref[x, y] = slope
        return carry[0] + slope, carry[1] + slope * normed

    zero = jnp.zeros((C, Z), F32)
    t_ref[...] = pack_pair(*rows(X, Y, step, (zero, zero)))


def last_kernel(p_ref, v_ref, w_ref, o_ref, dw_ref, acc_ref, own_ref):
    X, Y, C, Z = o_ref.shape
    fill_own(v_ref, own_ref)
    conv_rows(p_ref, w_ref, acc_ref, own_ref, dw_ref)

    def step(x, y, carry):
        o_ref[x, y] = acc_ref[x, y + 2].astype(BF16)
        return carry

    rows(X, Y, step, 0)


def call(kernel, name, outs, *operands, scratch=()):
    return pl.pallas_call(
        kernel,
        name=name,
        out_shape=[jax.ShapeDtypeStruct(s, d) for s, d in outs],
        in_specs=[VSPEC] * len(operands),
        out_specs=[VSPEC] * len(outs),
        scratch_shapes=[pltpu.VMEM(s, d) for s, d in scratch],
    )(*operands)


def local(features, kernel_one, gain_one, bias_one, kernel_two, gain_two, bias_two, cotangent):
    C, X, Y, Z = features.shape
    nx, ny = lax.axis_size("gx"), lax.axis_size("gy")
    total_cells = float(X * Y * Z * nx * ny)
    full = (X, Y, C, Z)
    tall = (X, Y + 4, C, Z)
    stat = (C, 128)

    def ahead(kernel):
        return jnp.transpose(kernel, (2, 3, 0, 4, 1)).reshape(9 * C, 3 * C)

    def behind(kernel):
        return jnp.transpose(kernel[:, :, ::-1, ::-1, ::-1], (2, 3, 1, 4, 0)).reshape(9 * C, 3 * C)

    def rows_of(gain, bias):
        return jnp.broadcast_to(jnp.stack([gain, bias])[:, :, None], (2, C, Z))

    params_one, params_two = rows_of(gain_one, bias_one), rows_of(gain_two, bias_two)
    ft = jnp.transpose(features, (1, 2, 0, 3))
    ct = jnp.transpose(cotangent, (1, 2, 0, 3))

    h1, s1 = call(
        forward_kernel, "forward", [(full, F32), (stat, F32)], halo(ft, nx, ny),
        ahead(kernel_one), scratch=[(tall, F32)],
    )
    s1 = sum_stats(s1, nx, ny)
    (a,) = call(
        functools.partial(active_kernel, total_cells), "active", [(full, BF16)], h1, s1, params_one
    )
    h2, s2 = call(
        forward_kernel, "forward", [(full, F32), (stat, F32)], halo(a, nx, ny),
        ahead(kernel_two), scratch=[(tall, F32)],
    )
    s2 = sum_stats(s2, nx, ny)
    out, t2 = call(
        functools.partial(output_kernel, total_cells), "output", [(full, BF16), (stat, F32)],
        h2, s2, params_two, ct,
    )
    t2 = sum_stats(t2, nx, ny)
    (g2,) = call(
        functools.partial(gradient_kernel, total_cells, False), "grad_two", [(full, BF16)],
        h2, s2, params_two, ct, t2,
    )
    slope_one, t1, dw2 = call(
        functools.partial(back_kernel, total_cells), "back",
        [(full, F32), (stat, F32), ((9 * C, 128), F32)],
        halo(g2, nx, ny), a, behind(kernel_two), h1, s1, params_one,
        scratch=[(tall, F32), (tall, BF16)],
    )
    t1 = sum_stats(t1, nx, ny)
    (g1,) = call(
        functools.partial(gradient_kernel, total_cells, True), "grad_one", [(full, BF16)],
        h1, s1, params_one, slope_one, t1,
    )
    fg, dw1 = call(
        last_kernel, "last", [(full, BF16), ((9 * C, 128), F32)],
        halo(g1, nx, ny), ft, behind(kernel_one), scratch=[(tall, F32), (tall, BF16)],
    )
    summed = sum_weights(jnp.concatenate([dw1, dw2], axis=0), nx, ny)
    scale = 1.0 / jnp.sqrt(jnp.float32(total_cells))

    def gradient_of(block):
        split = block[:, : 3 * C].reshape(3, 3, C, 3, C)
        return jnp.transpose(split[::-1, :, :, ::-1, :], (4, 2, 0, 1, 3)) * scale

    norm_grads = jnp.stack([t1[:, 1], t1[:, 0], t2[:, 1], t2[:, 0]]) * scale
    return (
        jnp.transpose(out, (2, 0, 1, 3)),
        jnp.transpose(fg, (2, 0, 1, 3)),
        gradient_of(summed[: 9 * C]),
        gradient_of(summed[9 * C :]),
        norm_grads,
    )


def solution(mesh):
    in_specs = (P(None, "gx", "gy", None), P(), P(), P(), P(), P(), P(), P(None, "gx", "gy", None))
    out_specs = (P(None, "gx", "gy", None), P(None, "gx", "gy", None), P(), P(), P())
    return jax.shard_map(local, mesh=mesh, in_specs=in_specs, out_specs=out_specs, check_vma=False)
```

time: 476 us -> 186 us (0.39); the launches traced: 467 us -> 185 us
  blocking collectives: 171 us -> 0 us
  Pallas kernels: 0 us -> 164 us
  waiting for transfers between devices: 154 us -> 0 us
  matrix products: 60.4 us -> 0 us
  starting transfers between devices: 30.8 us -> 0 us
  other arithmetic: 25.5 us -> 1.65 us
  between operations: 15.7 us -> 0.95 us
  local copies, waits for them, and re-layouts: 9.54 us -> 18.9 us
    psum x4 -> x0, blocking collectives: 171 us -> none  [the longest x2 87.7 us: channel_stats(): lax.psum((jnp.sum(hidden, axis=(1, 2, 3)), jnp.sum(jnp.square(hidden), ax...]
    pallas_call x0 -> x17, Pallas kernels: none -> 164 us  [the longest x4 56.4 us: halo(): pl.pallas_call(functools.partial(halo_kernel, nx, ny), name='halo', out_s...]
    psum x1 -> x0, waiting for transfers between devices: 133 us -> none  [sum_weights(): return lax.psum(local_terms, ('gx', 'gy'))]
    dot_general x162 -> x0, matrix products: 60.4 us -> none  [the longest x108 43.5 us: conv_valid(): jnp.einsum('oi,ixyz->oxyz', kernel[:, :, off_x, off_y, off_z], window, pr...]
    ppermute x16 -> x0, starting transfers between devices: 30.8 us -> none  [the longest x8 20 us: extended(): lax.ppermute(lax.slice_in_dim(block, block.shape[dim] - width, None, axis...]
    ppermute x16 -> x0, waiting for transfers between devices: 20.7 us -> none  [the longest x8 20.7 us: extended(): lax.ppermute(lax.slice_in_dim(block, 0, width, axis=dim), axis, backward)]
    concatenate x7 -> x1, other arithmetic: 8.05 us -> 0.73 us  [local(): summed = sum_weights(jnp.concatenate([dw1, dw2], axis=0), nx, ny)]
    convert_element_type x3 -> x0, other arithmetic: 5.97 us -> none  [the longest x2 3.82 us: norm_backward(): return (gradient.astype(jnp.bfloat16), sum_plain, sum_normed)]
  transfers between devices with their start and end apart: 17 -> 0, of which waited for: 7 -> 0; matrix products, arithmetic and copies ran while one was open for 4% -> 0% of each run, Pallas kernels for 0% -> 0%
where the time goes in v1:
time: 186 us; the launch traced here: 185 us
  Pallas kernels  164 us (88%)
  local copies, waits for them, and re-layouts  18.9 us (10%)
    pallas_call x4, Pallas kernels, halo(): pl.pallas_call(functools.partial(halo_kernel, nx, ny), name='halo', out_s...  56.4 us
    pallas_call x8, Pallas kernels, call(): pl.pallas_call(kernel, name=name, out_shape=[jax.ShapeDtypeStruct(s, d) f...  48.9 us
    pallas_call x4, Pallas kernels, sum_stats(): pl.pallas_call(functools.partial(stats_kernel, nx, ny), name='stats_sum',...  41.8 us
    pallas_call x1, Pallas kernels, sum_weights(): pl.pallas_call(functools.partial(weights_kernel, nx, ny), name='weights_s...  16.9 us
    unnamed x28, local copies, waits for them, and re-layouts  9.43 us

profile of v1, /device:TPU:0, one launch (start us, length us, event | category | flops | bytes accessed | tf_op | source)
XLA Modules:
  0.0 185.4 jit_solution(16937145518607857217)
XLA Ops:
  0.6 0.0 copy-start.1
  0.6 2.2 %copy.34 = bf16[32,2,32,128]{3,0,2,1:T(8,128)(2,1)} copy(bf16[32,2,32,128]{3,2,1,0:T(8,128)(2,1)} %param.8) | data formatting | bytes 1048576 | tf_op args[0]
  2.9 16.0 %halo.4.p_ref = bf16[4,34,32,128]{3,2,1,0:T(8,128)(2,1)} custom-call(bf16[2,32,32,128]{3,2,1,0:T(8,128)(2,1)} %bitcast.31), custom_call_target="tpu_custom_call" | custom-call | tf_op jit(solution)/shard_map/halo/pallas_call | solution.py:80
  18.9 0.0 copy-start.7
  18.9 0.0 copy-start.8
  18.9 0.0 copy-done.1
  18.9 0.2 copy.22
  19.1 0.8 reshape.36.w_ref
  19.9 7.5 %forward.2 = (f32[2,32,32,128]{3,2,1,0:T(8,128)}, f32[32,128]{1,0:T(8,128)}) custom-call(bf16[4,34,32,128]{3,2,1,0:T(8,128)(2,1)} %halo.4.p_ref, bf16[288,96]{1,0:T(8,128)(2,1)} %reshape.36.w_ref), custom_call_target="tpu_custom_call" | custom-call | tf_op jit(solution)/shard_map/forward/pallas_call | solution.py:391
  27.3 10.8 %stats_sum.4.s_ref = f32[32,128]{1,0:T(8,128)} custom-call(f32[32,128]{1,0:T(8,128)} %get-tuple-element.17.s_ref), custom_call_target="tpu_custom_call" | custom-call | tf_op jit(solution)/shard_map/stats_sum/pallas_call | solution.py:154
  38.2 0.0 copy-done.7
  38.2 0.0 copy-done.8
  38.2 0.7 broadcast_in_dim.4.gb_ref
  38.9 3.6 %active.1.t_ref.v_ref = bf16[2,32,32,128]{3,2,1,0:T(8,128)(2,1)} custom-call(f32[2,32,32,128]{3,2,1,0:T(8,128)} %get-tuple-element.16.h_ref, f32[32,128]{1,0:T(8,128)} %stats_sum.4.s_ref, f32[2,32,128]{2,1,0:T(8,128)} %broadcast_in_dim.4.gb_ref), custom_call_target="tpu_custom_call" | custom-call | tf_op jit(solution)/shard_map/active/pallas_call | solution.py:391
  42.5 0.0 copy-start
  42.5 13.3 %halo.5.p_ref = bf16[4,34,32,128]{3,2,1,0:T(8,128)(2,1)} custom-call(bf16[2,32,32,128]{3,2,1,0:T(8,128)(2,1)} %active.1.t_ref.v_ref), custom_call_target="tpu_custom_call" | custom-call | tf_op jit(solution)/shard_map/halo/pallas_call | solution.py:80
  55.8 0.0 copy-start.9
  55.9 0.0 copy-start.10
  55.9 0.0 copy-start.2
  55.9 0.0 copy-done
  55.9 0.2 copy.23
  56.1 0.8 reshape.37.w_ref
  56.9 7.5 %forward.3 = (f32[2,32,32,128]{3,2,1,0:T(8,128)}, f32[32,128]{1,0:T(8,128)}) custom-call(bf16[4,34,32,128]{3,2,1,0:T(8,128)(2,1)} %halo.5.p_ref, bf16[288,96]{1,0:T(8,128)(2,1)} %reshape.37.w_ref), custom_call_target="tpu_custom_call" | custom-call | tf_op jit(solution)/shard_map/forward/pallas_call | solution.py:391
  64.3 10.1 %stats_sum.5.s_ref = f32[32,128]{1,0:T(8,128)} custom-call(f32[32,128]{1,0:T(8,128)} %get-tuple-element.19.s_ref), custom_call_target="tpu_custom_call" | custom-call | tf_op jit(solution)/shard_map/stats_sum/pallas_call | solution.py:154
  74.4 0.0 copy-done.9
  74.4 0.0 copy-done.10
  74.4 0.7 broadcast_in_dim.5.gb_ref
  75.1 0.0 copy-done.2
  75.1 1.1 copy.33
  76.3 4.2 %output.1 = (bf16[2,32,32,128]{3,2,1,0:T(8,128)(2,1)}, f32[32,128]{1,0:T(8,128)}) custom-call(f32[2,32,32,128]{3,2,1,0:T(8,128)} %get-tuple-element.18.h_ref, f32[32,128]{1,0:T(8,128)} %stats_sum.5.s_ref, f32[2,32,128]{2,1,0:T(8,128)} %broadcast_in_dim.5.gb_ref, bf16[2,32,32,128]{3,2,1,0:T(8,128)(2,1)} %bitcast.33), custom_call_target="tpu_custom_call" | custom-call | tf_op jit(solution)/shard_map/output/pallas_call | solution.py:391
  80.4 2.0 %copy.27 = bf16[32,2,32,128]{3,2,1,0:T(8,128)(2,1)} copy(bf16[32,2,32,128]{3,0,2,1:T(8,128)(2,1)} %bitcast.41) | data formatting | bytes 1048576
  82.5 10.9 %stats_sum.6.t_ref = f32[32,128]{1,0:T(8,128)} custom-call(f32[32,128]{1,0:T(8,128)} %get-tuple-element.21.s_ref), custom_call_target="tpu_custom_call" | custom-call | tf_op jit(solution)/shard_map/stats_sum/pallas_call | solution.py:154
  93.3 3.6 %grad_two.1.t_ref = bf16[2,32,32,128]{3,2,1,0:T(8,128)(2,1)} custom-call(f32[2,32,32,128]{3,2,1,0:T(8,128)} %get-tuple-element.18.h_ref, f32[32,128]{1,0:T(8,128)} %stats_sum.5.s_ref, f32[2,32,128]{2,1,0:T(8,128)} %broadcast_in_dim.5.gb_ref, bf16[2,32,32,128]{3,2,1,0:T(8,128)(2,1)} %bitcast.34, f32[32,128]{1,0:T(8,128)} %stats_sum.6.t_ref), custom_call_target="tpu_custom_call" | custom-call | tf_op jit(solution)/shard_map/grad_two/pallas_call | solution.py:391
  96.9 13.4 %halo.6.p_ref = bf16[4,34,32,128]{3,2,1,0:T(8,128)(2,1)} custom-call(bf16[2,32,32,128]{3,2,1,0:T(8,128)(2,1)} %grad_two.1.t_ref), custom_call_target="tpu_custom_call" | custom-call | tf_op jit(solution)/shard_map/halo/pallas_call | solution.py:80
  110.4 0.2 copy.25
  110.6 0.8 reshape.38.w_ref
  111.4 10.4 %back.1 = (f32[2,32,32,128]{3,2,1,0:T(8,128)}, f32[32,128]{1,0:T(8,128)}, f32[288,128]{1,0:T(8,128)}) custom-call(bf16[4,34,32,128]{3,2,1,0:T(8,128)(2,1)} %halo.6.p_ref, bf16[2,32,32,128]{3,2,1,0:T(8,128)(2,1)} %active.1.t_ref.v_ref, bf16[288,96]{1,0:T(8,128)(2,1)} %reshape.38.w_ref, f32[2,32,32,128]{3,2,1,0:T(8,128)} %get-tuple-element.16.h_ref, ...), custom_call_target="tpu_custom_call" | custom-call | tf_op jit(solution)/shard_map/back/pallas_call | solution.py:391
  121.8 10.1 %stats_sum.7.t_ref = f32[32,128]{1,0:T(8,128)} custom-call(f32[32,128]{1,0:T(8,128)} %get-tuple-element.23.s_ref), custom_call_target="tpu_custom_call" | custom-call | tf_op jit(solution)/shard_map/stats_sum/pallas_call | solution.py:154
  131.9 3.4 %grad_one.1.t_ref = bf16[2,32,32,128]{3,2,1,0:T(8,128)(2,1)} custom-call(f32[2,32,32,128]{3,2,1,0:T(8,128)} %get-tuple-element.16.h_ref, f32[32,128]{1,0:T(8,128)} %stats_sum.4.s_ref, f32[2,32,128]{2,1,0:T(8,128)} %broadcast_in_dim.4.gb_ref, f32[2,32,32,128]{3,2,1,0:T(8,128)} %get-tuple-element.22.c_ref, f32[32,128]{1,0:T(8,128)} %stats_sum.7.t_ref), custom_call_target="tpu_custom_call" | custom-call | tf_op jit(solution)/shard_map/grad_one/pallas_call | solution.py:391
  135.2 13.6 %halo.7.p_ref = bf16[4,34,32,128]{3,2,1,0:T(8,128)(2,1)} custom-call(bf16[2,32,32,128]{3,2,1,0:T(8,128)(2,1)} %grad_one.1.t_ref), custom_call_target="tpu_custom_call" | custom-call | tf_op jit(solution)/shard_map/halo/pallas_call | solution.py:80
  148.9 0.2 copy.26
  149.1 0.8 reshape.39.w_ref
  149.9 8.8 %last.1 = (bf16[2,32,32,128]{3,2,1,0:T(8,128)(2,1)}, f32[288,128]{1,0:T(8,128)}) custom-call(bf16[4,34,32,128]{3,2,1,0:T(8,128)(2,1)} %halo.7.p_ref, bf16[2,32,32,128]{3,2,1,0:T(8,128)(2,1)} %bitcast.32, bf16[288,96]{1,0:T(8,128)(2,1)} %reshape.39.w_ref), custom_call_target="tpu_custom_call" | custom-call | tf_op jit(solution)/shard_map/last/pallas_call | solution.py:391
  158.7 2.1 %copy.28 = bf16[32,2,32,128]{3,2,1,0:T(8,128)(2,1)} copy(bf16[32,2,32,128]{3,0,2,1:T(8,128)(2,1)} %bitcast.40) | data formatting | bytes 1048576
  160.8 0.0 copy-done.5
  160.8 0.0 copy-done.6
  160.8 0.7 pad_maximum_fusion
  161.5 16.9 %weights_sum.1 = f32[8,72,128]{2,1,0:T(8,128)} custom-call(f32[8,72,128]{2,1,0:T(8,128)} %bitcast.35), custom_call_target="tpu_custom_call" | custom-call | tf_op jit(solution)/shard_map/weights_sum/pallas_call | solution.py:191
  178.4 1.0 fusion
  179.4 0.2 reshape.41
  179.6 1.1 rev.14
  180.8 0.1 multiply_bitcast_fusion.1
  180.9 1.0 copy.29
  181.9 0.2 reshape.42
  182.1 1.1 rev.15
  183.3 0.0 copy-start.3
  183.3 0.0 copy-start.4
  183.3 0.1 multiply_bitcast_fusion
  183.5 1.0 copy.30
  184.4 0.0 copy-done.3
  184.4 0.2 slice_reduce_fusion.1
  184.6 0.0 copy-done.4
  184.6 0.2 slice_reduce_fusion.3
  184.8 0.6 maximum_multiply_fusion
  (6 shorter events, 0.1 us)
Async XLA Ops:
  0.6 18.3 %copy-start.1 = (bf16[32,32,3,3,3]{1,0,4,3,2:T(8,128)(2,1)S(1)}, bf16[32,32,3,3,3]{1,0,4,3,2:T(8,128)(2,1)}, u32[]{:S(2)}) copy-start(bf16[32,32,3,3,3]{1,0,4,3,2:T(8,128)(2,1)} %param.9) | copy-start | bytes 165892
  18.9 19.3 %copy-start.7 = (f32[32]{0:T(128)S(1)}, f32[32]{0:T(128)}, u32[]{:S(2)}) copy-start(f32[32]{0:T(128)} %param.11) | copy-start | bytes 388
  18.9 19.3 %copy-start.8 = (f32[32]{0:T(128)S(1)}, f32[32]{0:T(128)}, u32[]{:S(2)}) copy-start(f32[32]{0:T(128)} %param.10) | copy-start | bytes 388
  42.5 13.4 %copy-start = (bf16[32,32,3,3,3]{1,0,4,3,2:T(8,128)(2,1)S(1)}, bf16[32,32,3,3,3]{1,0,4,3,2:T(8,128)(2,1)}, u32[]{:S(2)}) copy-start(bf16[32,32,3,3,3]{1,0,4,3,2:T(8,128)(2,1)} %param.12) | copy-start | bytes 165892
  55.8 18.6 %copy-start.9 = (f32[32]{0:T(128)S(1)}, f32[32]{0:T(128)}, u32[]{:S(2)}) copy-start(f32[32]{0:T(128)} %param.14) | copy-start | bytes 388
  55.9 18.6 %copy-start.10 = (f32[32]{0:T(128)S(1)}, f32[32]{0:T(128)}, u32[]{:S(2)}) copy-start(f32[32]{0:T(128)} %param.13) | copy-start | bytes 388
  55.9 19.3 %copy-start.2 = (bf16[32,2,32,128]{3,2,1,0:T(8,128)(2,1)S(1)}, bf16[32,2,32,128]{3,2,1,0:T(8,128)(2,1)}, u32[]{:S(2)}) copy-start(bf16[32,2,32,128]{3,2,1,0:T(8,128)(2,1)} %param.15) | copy-start | bytes 1572868
  149.9 10.9 %copy-start.5 = (f32[288,128]{1,0:T(8,128)S(1)}, f32[288,128]{1,0:T(8,128)}, u32[]{:S(2)}) copy-start(f32[288,128]{1,0:T(8,128)} %get-tuple-element.26) | copy-start | bytes 442372
  158.7 2.1 %copy-start.6 = (f32[288,128]{1,0:T(8,128)S(1)}, f32[288,128]{1,0:T(8,128)}, u32[]{:S(2)}) copy-start(f32[288,128]{1,0:T(8,128)} %get-tuple-element.25) | copy-start | bytes 442372
  183.3 1.1 copy-start.3
  183.3 1.3 copy-start.4

commit v2 on v1

--- a/solution.py
+++ b/solution.py
@@ -14,6 +14,7 @@
 F32 = jnp.float32
 BF16 = jnp.bfloat16
 VSPEC = pl.BlockSpec(memory_space=pltpu.VMEM)
+PIECES = 4
 DIRECTIONS = [(i, j) for i in (-1, 0, 1) for j in (-1, 0, 1) if (i, j) != (0, 0)]
 
 
@@ -27,7 +28,7 @@
     return SLOPE + (1.0 - SLOPE) / (1.0 + jnp.exp(-SHARPNESS * shifted))
 
 
-def halo_kernel(nx, ny, t_ref, o_ref, p_ref, send, recv):
+def start_halo(nx, ny, t_ref, p_ref, send, recv):
     gx, gy = lax.axis_index("gx"), lax.axis_index("gy")
     X, Y = t_ref.shape[0], t_ref.shape[1]
     peers = [(lax.rem(gx + dx + nx, nx), lax.rem(gy + dy + ny, ny)) for dx, dy in DIRECTIONS]
@@ -42,54 +43,28 @@
     def target(d, size):
         return pl.ds(0, 1) if d == 1 else (pl.ds(size + 1, 1) if d == -1 else pl.ds(1, size))
 
-    copies = []
-    for k, (dx, dy) in enumerate(DIRECTIONS):
+    piece = Y // PIECES
+    plan = []
+    for n in range(PIECES):
+        for k, (dx, dy) in enumerate(DIRECTIONS):
+            if dy == 0:
+                rows_from, rows_to = pl.ds(n * piece, piece), pl.ds(n * piece + 1, piece)
+                plan.append((n, k, dx, rows_from, rows_to))
+            elif n == 0:
+                plan.append((n, k, dx, source(dy, Y), target(dy, Y)))
+    groups = [[] for _ in range(PIECES)]
+    for index, (n, k, dx, rows_from, rows_to) in enumerate(plan):
         copy = pltpu.make_async_remote_copy(
-            src_ref=t_ref.at[source(dx, X), source(dy, Y)],
-            dst_ref=p_ref.at[target(dx, X), target(dy, Y)],
-            send_sem=send.at[k],
-            recv_sem=recv.at[k],
+            src_ref=t_ref.at[source(dx, X), rows_from],
+            dst_ref=p_ref.at[target(dx, X), rows_to],
+            send_sem=send.at[index],
+            recv_sem=recv.at[index],
             device_id=peers[k],
             device_id_type=MESH,
         )
         copy.start()
-        copies.append(copy)
-    o_ref[1 : X + 1, 1 : Y + 1] = t_ref[...]
-    for copy in copies:
-        copy.wait()
-    low_x = jnp.where(gx > 0, 1.0, 0.0)
-    high_x = jnp.where(gx < nx - 1, 1.0, 0.0)
-    low_y = jnp.where(gy > 0, 1.0, 0.0)
-    high_y = jnp.where(gy < ny - 1, 1.0, 0.0)
-
-    def kept(values, flag):
-        return (values.astype(F32) * flag).astype(BF16)
-
-    o_ref[0, 1 : Y + 1] = kept(p_ref[0, 1 : Y + 1], low_x)
-    o_ref[X + 1, 1 : Y + 1] = kept(p_ref[X + 1, 1 : Y + 1], high_x)
-    for x in range(X + 2):
-        side = low_x if x == 0 else (high_x if x == X + 1 else None)
-        low = low_y if side is None else low_y * side
-        high = high_y if side is None else high_y * side
-        o_ref[x, 0] = kept(p_ref[x, 0], low)
-        o_ref[x, Y + 1] = kept(p_ref[x, Y + 1], high)
-
-
-def halo(block, nx, ny):
-    X, Y, C, Z = block.shape
-    return pl.pallas_call(
-        functools.partial(halo_kernel, nx, ny),
-        name="halo",
-        out_shape=jax.ShapeDtypeStruct((X + 2, Y + 2, C, Z), block.dtype),
-        in_specs=[VSPEC],
-        out_specs=VSPEC,
-        scratch_shapes=[
-            pltpu.VMEM((X + 2, Y + 2, C, Z), block.dtype),
-            pltpu.SemaphoreType.DMA((8,)),
-            pltpu.SemaphoreType.DMA((8,)),
-        ],
-        compiler_params=pltpu.CompilerParams(collective_id=0, has_side_effects=True),
-    )(block)
+        groups[n].append(copy)
+    return groups
 
 
 def greet(nx, ny, gx, gy):
@@ -212,66 +187,122 @@
     return summed.reshape(nx * piece, L)[:R]
 
 
-def taps(row):
+def taps(row, flip, keep=None):
     wide = row.astype(F32)
+    if keep is not None:
+        wide = wide * keep
+        row = wide.astype(BF16)
     size = row.shape[1]
     lane = lax.broadcasted_iota(jnp.int32, wide.shape, 1)
     before = jnp.where(lane == 0, 0.0, pltpu.roll(wide, 1, 1)).astype(BF16)
     after = jnp.where(lane == size - 1, 0.0, pltpu.roll(wide, size - 1, 1)).astype(BF16)
-    return jnp.concatenate([before, row, after], axis=0)
-
-
-def conv_rows(p_ref, w_ref, acc_ref, v_ref=None, dw_ref=None):
-    X = acc_ref.shape[0]
-    C = acc_ref.shape[2]
-    Z = acc_ref.shape[3]
+    return jnp.concatenate([after, row, before] if flip else [before, row, after], axis=0)
+
+
+def conv_halo(nx, ny, flip, t_ref, w_ref, acc_ref, p_ref, send, recv, v_ref=None, dw_ref=None):
+    X, _, C, Z = acc_ref.shape
+    Y = t_ref.shape[1]
+    gx, gy = lax.axis_index("gx"), lax.axis_index("gy")
+    groups = start_halo(nx, ny, t_ref, p_ref, send, recv)
     acc_ref[...] = jnp.zeros_like(acc_ref)
     if dw_ref is not None:
-        dw_ref[...] = jnp.zeros_like(dw_ref)
-
-    def body(j, carry):
+        dw_ref[...] = jnp.zeros(dw_ref.shape, F32)
+
+    def pair_step(xp, ya, yb, tap_a, tap_b):
+        first, last = max(0, xp - (X - 1)), min(2, xp)
+        blocks = range(2 - last, 3 - first) if flip else range(first, last + 1)
+        low, high = blocks[0] * 3 * C, (blocks[-1] + 1) * 3 * C
+        pair = jnp.concatenate([tap_a, tap_b], axis=1)
+        part = jnp.dot(w_ref[low:high, :], pair, preferred_element_type=F32)
+        left = []
+        for n, block in enumerate(blocks):
+            x = xp - 2 + block if flip else xp - block
+            base = n * 3 * C
+            one = [part[base + d * C : base + (d + 1) * C, :Z] for d in range(3)]
+            two = [part[base + d * C : base + (d + 1) * C, Z:] for d in range(3)]
+            if not flip:
+                one, two = one[::-1], two[::-1]
+            if yb is None:
+                acc_ref[x, ya] += one[0]
+                acc_ref[x, ya + 1] += one[1] + two[0]
+                acc_ref[x, ya + 2] += one[2] + two[1]
+                acc_ref[x, ya + 3] += two[2]
+            else:
+                for d in range(3):
+                    acc_ref[x, ya + d] += one[d]
+                for d in range(3):
+                    acc_ref[x, yb + d] += two[d]
+            if dw_ref is not None:
+                second = ya + 1 if yb is None else yb
+                now = v_ref[x, pl.ds(ya, 3)].reshape(3 * C, Z)
+                later = v_ref[x, pl.ds(second, 3)].reshape(3 * C, Z)
+                left.append(jnp.concatenate([now, later], axis=1))
+        if dw_ref is not None:
+            left = left[0] if len(left) == 1 else jnp.concatenate(left, axis=0)
+            dw_ref[low:high, : 3 * C] += lax.dot_general(
+                left, pair, (((1,), (1,)), ((), ())), preferred_element_type=F32
+            )
+
+    def inner(j, carry):
+        y = 2 * j + 1
+        for xp in range(1, X + 1):
+            tap_a = taps(t_ref[xp - 1, y - 1], flip)
+            tap_b = taps(t_ref[xp - 1, y], flip)
+            pair_step(xp, y, None, tap_a, tap_b)
+        return carry
+
+    lax.fori_loop(0, Y // 2, inner, 0)
+    for copy in groups[0]:
+        copy.wait()
+    low_y = jnp.where(gy > 0, 1.0, 0.0)
+    high_y = jnp.where(gy < ny - 1, 1.0, 0.0)
+    for xp in range(1, X + 1):
+        tap_a = taps(p_ref[xp, 0], flip, low_y)
+        tap_b = taps(p_ref[xp, Y + 1], flip, high_y)
+        pair_step(xp, 0, Y + 1, tap_a, tap_b)
+    low_x = jnp.where(gx > 0, 1.0, 0.0)
+    high_x = jnp.where(gx < nx - 1, 1.0, 0.0)
+
+    def outer(j, carry):
         y = 2 * j
-        for xp in range(X + 2):
-            first, last = max(0, xp - (X - 1)), min(2, xp)
-            pair = jnp.concatenate([taps(p_ref[xp, y]), taps(p_ref[xp, y + 1])], axis=1)
-            part = jnp.dot(
-                w_ref[first * 3 * C : (last + 1) * 3 * C, :], pair, preferred_element_type=F32
-            )
-            for dx in range(first, last + 1):
-                base = (dx - first) * 3 * C
-                one = [part[base + d * C : base + (d + 1) * C, :Z] for d in range(3)]
-                two = [part[base + d * C : base + (d + 1) * C, Z:] for d in range(3)]
-                x = xp - dx
-                acc_ref[x, y] += one[2]
-                acc_ref[x, y + 1] += one[1] + two[2]
-                acc_ref[x, y + 2] += one[0] + two[1]
-                acc_ref[x, y + 3] += two[0]
-            if dw_ref is not None:
-                left = []
-                for dx in range(first, last + 1):
-                    x = xp - dx
-                    now = v_ref[x, pl.ds(y, 3)].reshape(3 * C, Z)
-                    later = v_ref[x, pl.ds(y + 1, 3)].reshape(3 * C, Z)
-                    left.append(jnp.concatenate([now, later], axis=1))
-                left = left[0] if len(left) == 1 else jnp.concatenate(left, axis=0)
-                dw_ref[first * 3 * C : (last + 1) * 3 * C, : 3 * C] += lax.dot_general(
-                    left, pair, (((1,), (1,)), ((), ())), preferred_element_type=F32
-                )
+        keep_a = jnp.where(y == 0, low_y, 1.0)
+        keep_b = jnp.where(y == Y, high_y, 1.0)
+        for xp, keep in ((0, low_x), (X + 1, high_x)):
+            tap_a = taps(p_ref[xp, y], flip, keep * keep_a)
+            tap_b = taps(p_ref[xp, y + 1], flip, keep * keep_b)
+            pair_step(xp, y, None, tap_a, tap_b)
         return carry
 
-    lax.fori_loop(0, p_ref.shape[1] // 2, body, 0)
+    done = 0
+    for n, group in enumerate(groups):
+        if n > 0:
+            for copy in group:
+                copy.wait()
+        ready = (Y + 2) // 2 if n == PIECES - 1 else (Y // PIECES * (n + 1) + 1) // 2
+        lax.fori_loop(done, ready, outer, 0)
+        done = ready
 
 
 def pack_pair(one, two):
+    C = one.shape[0]
     lane = lax.broadcasted_iota(jnp.int32, one.shape, 1)
     one = jnp.sum(one, axis=1, keepdims=True)
     two = jnp.sum(two, axis=1, keepdims=True)
-    return jnp.where(lane == 0, one, jnp.where(lane == 1, two, 0.0))
-
-
-def normal_terms(s_ref, total_cells):
-    center = s_ref[:, 0:1] / total_cells
-    spread_ = s_ref[:, 1:2] / total_cells - jnp.square(center)
+    tall = jnp.where(lane == 0, one, jnp.where(lane == 1, two, 0.0))
+    square = jnp.concatenate([tall, jnp.zeros((128 - C, 128), F32)], axis=0)
+    return jnp.transpose(square)[0:8]
+
+
+def unpack_pair(s_ref, C):
+    square = jnp.concatenate([s_ref[...], jnp.zeros((120, 128), F32)], axis=0)
+    tall = jnp.transpose(square)
+    return tall[:C, 0:1], tall[:C, 1:2]
+
+
+def normal_terms(s_ref, C, total_cells):
+    sums, squares = unpack_pair(s_ref, C)
+    center = sums / total_cells
+    spread_ = squares / total_cells - jnp.square(center)
     return center, lax.rsqrt(spread_ + EPSILON)
 
 
@@ -287,9 +318,9 @@
     return lax.fori_loop(0, Y // group, body, carry)
 
 
-def forward_kernel(p_ref, w_ref, h_ref, s_ref, acc_ref):
+def forward_kernel(nx, ny, t_ref, w_ref, h_ref, s_ref, acc_ref, p_ref, send, recv):
     X, Y, C, Z = h_ref.shape
-    conv_rows(p_ref, w_ref, acc_ref)
+    conv_halo(nx, ny, False, t_ref, w_ref, acc_ref, p_ref, send, recv)
 
     def step(x, y, carry):
         h = acc_ref[x, y + 2]
@@ -302,7 +333,7 @@
 
 def active_kernel(total_cells, h_ref, s_ref, gb_ref, a_ref):
     X, Y, C, Z = h_ref.shape
-    center, inverse = normal_terms(s_ref, total_cells)
+    center, inverse = normal_terms(s_ref, C, total_cells)
     gain, bias = gb_ref[0], gb_ref[1]
 
     def step(x, y, carry):
@@ -315,7 +346,7 @@
 
 def output_kernel(total_cells, h_ref, s_ref, gb_ref, c_ref, o_ref, t_ref):
     X, Y, C, Z = h_ref.shape
-    center, inverse = normal_terms(s_ref, total_cells)
+    center, inverse = normal_terms(s_ref, C, total_cells)
     gain, bias = gb_ref[0], gb_ref[1]
 
     def step(x, y, carry):
@@ -331,10 +362,9 @@
 
 def gradient_kernel(total_cells, has_slope, h_ref, s_ref, gb_ref, c_ref, t_ref, g_ref):
     X, Y, C, Z = h_ref.shape
-    center, inverse = normal_terms(s_ref, total_cells)
+    center, inverse = normal_terms(s_ref, C, total_cells)
     gain, bias = gb_ref[0], gb_ref[1]
-    plain = t_ref[:, 0:1] / total_cells
-    along = t_ref[:, 1:2] / total_cells
+    plain, along = [v / total_cells for v in unpack_pair(t_ref, C)]
     factor = gain * inverse
 
     def step(x, y, carry):
@@ -357,12 +387,13 @@
 
 
 def back_kernel(
-    total_cells, p_ref, v_ref, w_ref, h_ref, s_ref, gb_ref, o_ref, t_ref, dw_ref, acc_ref, own_ref
+    total_cells, nx, ny, g_ref, v_ref, w_ref, h_ref, s_ref, gb_ref,
+    o_ref, t_ref, dw_ref, acc_ref, p_ref, send, recv, own_ref,
 ):
     X, Y, C, Z = o_ref.shape
     fill_own(v_ref, own_ref)
-    conv_rows(p_ref, w_ref, acc_ref, own_ref, dw_ref)
-    center, inverse = normal_terms(s_ref, total_cells)
+    conv_halo(nx, ny, True, g_ref, w_ref, acc_ref, p_ref, send, recv, own_ref, dw_ref)
+    center, inverse = normal_terms(s_ref, C, total_cells)
     gain, bias = gb_ref[0], gb_ref[1]
 
     def step(x, y, carry):
@@ -375,10 +406,14 @@
     t_ref[...] = pack_pair(*rows(X, Y, step, (zero, zero)))
 
 
-def last_kernel(p_ref, v_ref, w_ref, o_ref, dw_ref, acc_ref, own_ref):
+def last_kernel(
+    nx, ny, g_ref, v_ref, w_ref, d_ref, o_ref, both_ref, acc_ref, p_ref, send, recv, own_ref
+):
     X, Y, C, Z = o_ref.shape
     fill_own(v_ref, own_ref)
-    conv_rows(p_ref, w_ref, acc_ref, own_ref, dw_ref)
+    both_ref[9 * C :] = d_ref[...]
+    dw_ref = both_ref.at[0 : 9 * C]
+    conv_halo(nx, ny, True, g_ref, w_ref, acc_ref, p_ref, send, recv, own_ref, dw_ref)
 
     def step(x, y, carry):
         o_ref[x, y] = acc_ref[x, y + 2].astype(BF16)
@@ -387,14 +422,20 @@
     rows(X, Y, step, 0)
 
 
-def call(kernel, name, outs, *operands, scratch=()):
+def call(kernel, name, outs, *operands, scratch=(), collective=None):
+    params = {}
+    if collective is not None:
+        params["compiler_params"] = pltpu.CompilerParams(
+            collective_id=collective, has_side_effects=True
+        )
     return pl.pallas_call(
         kernel,
         name=name,
         out_shape=[jax.ShapeDtypeStruct(s, d) for s, d in outs],
         in_specs=[VSPEC] * len(operands),
         out_specs=[VSPEC] * len(outs),
-        scratch_shapes=[pltpu.VMEM(s, d) for s, d in scratch],
+        scratch_shapes=list(scratch),
+        **params,
     )(*operands)
 
 
@@ -404,13 +445,21 @@
     total_cells = float(X * Y * Z * nx * ny)
     full = (X, Y, C, Z)
     tall = (X, Y + 4, C, Z)
-    stat = (C, 128)
+    stat = (8, 128)
+    faces = [
+        pltpu.VMEM(tall, F32),
+        pltpu.VMEM((X + 2, Y + 2, C, Z), BF16),
+        pltpu.SemaphoreType.DMA((6 + 2 * PIECES,)),
+        pltpu.SemaphoreType.DMA((6 + 2 * PIECES,)),
+    ]
+    own = [pltpu.VMEM(tall, BF16)]
+    forward = functools.partial(forward_kernel, nx, ny)
 
     def ahead(kernel):
         return jnp.transpose(kernel, (2, 3, 0, 4, 1)).reshape(9 * C, 3 * C)
 
     def behind(kernel):
-        return jnp.transpose(kernel[:, :, ::-1, ::-1, ::-1], (2, 3, 1, 4, 0)).reshape(9 * C, 3 * C)
+        return jnp.transpose(kernel, (2, 3, 1, 4, 0)).reshape(9 * C, 3 * C)
 
     def rows_of(gain, bias):
         return jnp.broadcast_to(jnp.stack([gain, bias])[:, :, None], (2, C, Z))
@@ -420,16 +469,16 @@
     ct = jnp.transpose(cotangent, (1, 2, 0, 3))
 
     h1, s1 = call(
-        forward_kernel, "forward", [(full, F32), (stat, F32)], halo(ft, nx, ny),
-        ahead(kernel_one), scratch=[(tall, F32)],
+        forward, "forward", [(full, F32), (stat, F32)], ft, ahead(kernel_one),
+        scratch=faces, collective=0,
     )
     s1 = sum_stats(s1, nx, ny)
     (a,) = call(
         functools.partial(active_kernel, total_cells), "active", [(full, BF16)], h1, s1, params_one
     )
     h2, s2 = call(
-        forward_kernel, "forward", [(full, F32), (stat, F32)], halo(a, nx, ny),
-        ahead(kernel_two), scratch=[(tall, F32)],
+        forward, "forward", [(full, F32), (stat, F32)], a, ahead(kernel_two),
+        scratch=faces, collective=0,
     )
     s2 = sum_stats(s2, nx, ny)
     out, t2 = call(
@@ -442,28 +491,28 @@
         h2, s2, params_two, ct, t2,
     )
     slope_one, t1, dw2 = call(
-        functools.partial(back_kernel, total_cells), "back",
+        functools.partial(back_kernel, total_cells, nx, ny), "back",
         [(full, F32), (stat, F32), ((9 * C, 128), F32)],
-        halo(g2, nx, ny), a, behind(kernel_two), h1, s1, params_one,
-        scratch=[(tall, F32), (tall, BF16)],
+        g2, a, behind(kernel_two), h1, s1, params_one,
+        scratch=faces + own, collective=3,
     )
     t1 = sum_stats(t1, nx, ny)
     (g1,) = call(
         functools.partial(gradient_kernel, total_cells, True), "grad_one", [(full, BF16)],
         h1, s1, params_one, slope_one, t1,
     )
-    fg, dw1 = call(
-        last_kernel, "last", [(full, BF16), ((9 * C, 128), F32)],
-        halo(g1, nx, ny), ft, behind(kernel_one), scratch=[(tall, F32), (tall, BF16)],
-    )
-    summed = sum_weights(jnp.concatenate([dw1, dw2], axis=0), nx, ny)
+    fg, dw = call(
+        functools.partial(last_kernel, nx, ny), "last", [(full, BF16), ((18 * C, 128), F32)],
+        g1, ft, behind(kernel_one), dw2, scratch=faces + own, collective=4,
+    )
+    summed = sum_weights(dw, nx, ny)
     scale = 1.0 / jnp.sqrt(jnp.float32(total_cells))
 
     def gradient_of(block):
         split = block[:, : 3 * C].reshape(3, 3, C, 3, C)
-        return jnp.transpose(split[::-1, :, :, ::-1, :], (4, 2, 0, 1, 3)) * scale
-
-    norm_grads = jnp.stack([t1[:, 1], t1[:, 0], t2[:, 1], t2[:, 0]]) * scale
+        return jnp.transpose(split, (4, 2, 0, 1, 3)) * scale
+
+    norm_grads = jnp.stack([t1[1, :C], t1[0, :C], t2[1, :C], t2[0, :C]]) * scale
     return (
         jnp.transpose(out, (2, 0, 1, 3)),
         jnp.transpose(fg, (2, 0, 1, 3)),

time: 186 us -> 155 us (0.83)
  Pallas kernels: 164 us -> 137 us
  local copies, waits for them, and re-layouts: 18.9 us -> 16.3 us
    pallas_call x4 -> x0, Pallas kernels: 56.4 us -> none  [halo(): pl.pallas_call(functools.partial(halo_kernel, nx, ny), name='halo', out_s...]
    pallas_call x8, Pallas kernels: 48.9 us -> 79.4 us  [call(): pl.pallas_call(kernel, name=name, out_shape=[jax.ShapeDtypeStruct(s, d) f...]
    rev x2 -> x0, local copies, waits for them, and re-layouts: 2.28 us -> none  [gradient_of(): return jnp.transpose(split[::-1, :, :, ::-1, :], (4, 2, 0, 1, 3)) * scale]
    unnamed x28 -> x24, local copies, waits for them, and re-layouts: 9.43 us -> 8.74 us
where the time goes in v2:
time: 155 us; the launch traced here: 154 us
  Pallas kernels  137 us (88%)
  local copies, waits for them, and re-layouts  16.3 us (11%)
    pallas_call x8, Pallas kernels, call(): pl.pallas_call(kernel, name=name, out_shape=[jax.ShapeDtypeStruct(s, d) f...  79.4 us
    pallas_call x4, Pallas kernels, sum_stats(): pl.pallas_call(functools.partial(stats_kernel, nx, ny), name='stats_sum',...  39.9 us
    pallas_call x1, Pallas kernels, sum_weights(): pl.pallas_call(functools.partial(weights_kernel, nx, ny), name='weights_s...  17.4 us
    unnamed x24, local copies, waits for them, and re-layouts  8.74 us

profile of v2, /device:TPU:0, one launch (start us, length us, event | category | flops | bytes accessed | tf_op | source)
XLA Modules:
  0.0 154.4 jit_solution(14142473574288473106)
XLA Ops:
  0.6 0.0 copy-start.1
  0.6 2.2 %copy.34 = bf16[32,2,32,128]{3,0,2,1:T(8,128)(2,1)} copy(bf16[32,2,32,128]{3,2,1,0:T(8,128)(2,1)} %param.8) | data formatting | bytes 1048576 | tf_op args[0]
  2.9 0.0 copy-done.1
  2.9 0.2 copy.22
  3.0 0.8 reshape.36.w_ref
  3.8 17.7 %forward.2 = (f32[2,32,32,128]{3,2,1,0:T(8,128)}, f32[8,128]{1,0:T(8,128)}) custom-call(bf16[2,32,32,128]{3,2,1,0:T(8,128)(2,1)} %bitcast.21, bf16[288,96]{1,0:T(8,128)(2,1)} %reshape.36.w_ref), custom_call_target="tpu_custom_call" | custom-call | tf_op jit(solution)/shard_map/forward/pallas_call | solution.py:431
  21.5 10.2 %stats_sum.4.s_ref = f32[8,128]{1,0:T(8,128)} custom-call(f32[8,128]{1,0:T(8,128)} %get-tuple-element.17.s_ref), custom_call_target="tpu_custom_call" | custom-call | tf_op jit(solution)/shard_map/stats_sum/pallas_call | solution.py:129
  31.7 0.0 copy-start.5
  31.7 0.0 copy-start.6
  31.7 0.6 copy-done.5
  32.3 0.0 copy-done.6
  32.4 0.7 broadcast_in_dim.4.gb_ref
  33.1 0.0 copy-start
  33.1 3.7 %active.1.t_ref.v_ref = bf16[2,32,32,128]{3,2,1,0:T(8,128)(2,1)} custom-call(f32[2,32,32,128]{3,2,1,0:T(8,128)} %get-tuple-element.16.h_ref, f32[8,128]{1,0:T(8,128)} %stats_sum.4.s_ref, f32[2,32,128]{2,1,0:T(8,128)} %broadcast_in_dim.4.gb_ref), custom_call_target="tpu_custom_call" | custom-call | tf_op jit(solution)/shard_map/active/pallas_call | solution.py:431
  36.8 0.0 copy-done
  36.8 0.2 copy.23
  36.9 0.0 copy-start.2
  36.9 0.8 reshape.37.w_ref
  37.7 14.5 %forward.3 = (f32[2,32,32,128]{3,2,1,0:T(8,128)}, f32[8,128]{1,0:T(8,128)}) custom-call(bf16[2,32,32,128]{3,2,1,0:T(8,128)(2,1)} %active.1.t_ref.v_ref, bf16[288,96]{1,0:T(8,128)(2,1)} %reshape.37.w_ref), custom_call_target="tpu_custom_call" | custom-call | tf_op jit(solution)/shard_map/forward/pallas_call | solution.py:431
  52.3 9.7 %stats_sum.5.s_ref = f32[8,128]{1,0:T(8,128)} custom-call(f32[8,128]{1,0:T(8,128)} %get-tuple-element.19.s_ref), custom_call_target="tpu_custom_call" | custom-call | tf_op jit(solution)/shard_map/stats_sum/pallas_call | solution.py:129
  62.0 0.0 copy-done.2
  62.0 1.2 copy.33
  63.1 0.0 copy-start.7
  63.1 0.0 copy-start.8
  63.1 0.7 copy-done.7
  63.8 0.0 copy-done.8
  63.8 0.7 broadcast_in_dim.5.gb_ref
  64.5 4.3 %output.1 = (bf16[2,32,32,128]{3,2,1,0:T(8,128)(2,1)}, f32[8,128]{1,0:T(8,128)}) custom-call(f32[2,32,32,128]{3,2,1,0:T(8,128)} %get-tuple-element.18.h_ref, f32[8,128]{1,0:T(8,128)} %stats_sum.5.s_ref, f32[2,32,128]{2,1,0:T(8,128)} %broadcast_in_dim.5.gb_ref, bf16[2,32,32,128]{3,2,1,0:T(8,128)(2,1)} %bitcast.23), custom_call_target="tpu_custom_call" | custom-call | tf_op jit(solution)/shard_map/output/pallas_call | solution.py:431
  68.8 10.3 %stats_sum.6.t_ref = f32[8,128]{1,0:T(8,128)} custom-call(f32[8,128]{1,0:T(8,128)} %get-tuple-element.21.s_ref), custom_call_target="tpu_custom_call" | custom-call | tf_op jit(solution)/shard_map/stats_sum/pallas_call | solution.py:129
  79.1 3.7 %grad_two.1.g_ref = bf16[2,32,32,128]{3,2,1,0:T(8,128)(2,1)} custom-call(f32[2,32,32,128]{3,2,1,0:T(8,128)} %get-tuple-element.18.h_ref, f32[8,128]{1,0:T(8,128)} %stats_sum.5.s_ref, f32[2,32,128]{2,1,0:T(8,128)} %broadcast_in_dim.5.gb_ref, bf16[2,32,32,128]{3,2,1,0:T(8,128)(2,1)} %bitcast.24, f32[8,128]{1,0:T(8,128)} %stats_sum.6.t_ref), custom_call_target="tpu_custom_call" | custom-call | tf_op jit(solution)/shard_map/grad_two/pallas_call | solution.py:431
  82.8 0.2 copy.25
  83.0 0.8 reshape.38.w_ref
  83.8 16.7 %back.1 = (f32[2,32,32,128]{3,2,1,0:T(8,128)}, f32[8,128]{1,0:T(8,128)}, f32[288,128]{1,0:T(8,128)}) custom-call(bf16[2,32,32,128]{3,2,1,0:T(8,128)(2,1)} %grad_two.1.g_ref, bf16[2,32,32,128]{3,2,1,0:T(8,128)(2,1)} %active.1.t_ref.v_ref, bf16[288,96]{1,0:T(8,128)(2,1)} %reshape.38.w_ref, f32[2,32,32,128]{3,2,1,0:T(8,128)} %get-tuple-element.16.h_ref, ...), custom_call_target="tpu_custom_call" | custom-call | tf_op jit(solution)/shard_map/back/pallas_call | solution.py:431
  100.5 9.7 %stats_sum.7.t_ref = f32[8,128]{1,0:T(8,128)} custom-call(f32[8,128]{1,0:T(8,128)} %get-tuple-element.23.s_ref), custom_call_target="tpu_custom_call" | custom-call | tf_op jit(solution)/shard_map/stats_sum/pallas_call | solution.py:129
  110.3 0.8 fusion.1
  111.0 0.6 maximum_multiply_fusion
  111.6 3.4 %grad_one.1.g_ref = bf16[2,32,32,128]{3,2,1,0:T(8,128)(2,1)} custom-call(f32[2,32,32,128]{3,2,1,0:T(8,128)} %get-tuple-element.16.h_ref, f32[8,128]{1,0:T(8,128)} %stats_sum.4.s_ref, f32[2,32,128]{2,1,0:T(8,128)} %broadcast_in_dim.4.gb_ref, f32[2,32,32,128]{3,2,1,0:T(8,128)} %get-tuple-element.22.c_ref, f32[8,128]{1,0:T(8,128)} %stats_sum.7.t_ref), custom_call_target="tpu_custom_call" | custom-call | tf_op jit(solution)/shard_map/grad_one/pallas_call | solution.py:431
  115.1 0.2 copy.26
  115.3 0.8 reshape.39.w_ref
  116.1 15.4 %last.1 = (bf16[2,32,32,128]{3,2,1,0:T(8,128)(2,1)}, f32[576,128]{1,0:T(8,128)}) custom-call(bf16[2,32,32,128]{3,2,1,0:T(8,128)(2,1)} %grad_one.1.g_ref, bf16[2,32,32,128]{3,2,1,0:T(8,128)(2,1)} %bitcast.22, bf16[288,96]{1,0:T(8,128)(2,1)} %reshape.39.w_ref, f32[288,128]{1,0:T(8,128)} %get-tuple-element.24.d_ref), custom_call_target="tpu_custom_call" | custom-call | tf_op jit(solution)/shard_map/last/pallas_call | solution.py:431
  131.5 17.4 %weights_sum.1 = f32[8,72,128]{2,1,0:T(8,128)} custom-call(f32[8,72,128]{2,1,0:T(8,128)} %bitcast.35), custom_call_target="tpu_custom_call" | custom-call | tf_op jit(solution)/shard_map/weights_sum/pallas_call | solution.py:166
  148.8 1.0 fusion
  149.9 0.2 mul.25
  150.1 1.0 copy.29
  151.1 0.2 mul.28
  151.3 0.0 copy-start.4
  151.3 1.0 copy.30
  152.3 0.1 copy-done.4
  152.4 0.0 copy-start.3
  152.4 1.0 copy.28
  153.4 0.0 copy-done.3
  153.4 1.0 copy.27
  (4 shorter events, 0.0 us)
Async XLA Ops:
  0.6 2.2 %copy-start.1 = (bf16[32,32,3,3,3]{1,0,4,3,2:T(8,128)(2,1)S(1)}, bf16[32,32,3,3,3]{1,0,4,3,2:T(8,128)(2,1)}, u32[]{:S(2)}) copy-start(bf16[32,32,3,3,3]{1,0,4,3,2:T(8,128)(2,1)} %param.9) | copy-start | bytes 165892
  31.7 0.7 copy-start.5
  31.7 0.7 copy-start.6
  33.1 3.7 %copy-start = (bf16[32,32,3,3,3]{1,0,4,3,2:T(8,128)(2,1)S(1)}, bf16[32,32,3,3,3]{1,0,4,3,2:T(8,128)(2,1)}, u32[]{:S(2)}) copy-start(bf16[32,32,3,3,3]{1,0,4,3,2:T(8,128)(2,1)} %param.12) | copy-start | bytes 165892
  36.9 25.0 %copy-start.2 = (bf16[32,2,32,128]{3,2,1,0:T(8,128)(2,1)S(1)}, bf16[32,2,32,128]{3,2,1,0:T(8,128)(2,1)}, u32[]{:S(2)}) copy-start(bf16[32,2,32,128]{3,2,1,0:T(8,128)(2,1)} %param.15) | copy-start | bytes 1572868
  63.1 0.7 copy-start.7
  63.1 0.7 copy-start.8
  151.3 1.0 copy-start.4
  152.4 1.0 copy-start.3
